TPU v7x, 128 devices: a whole 4x4x4 slice. The times are simulated.
128 devices in a mesh: section: 2 (over y_hi), dp: 64 (over z, x, y_lo, core).
Axes of the slice: x: 4, y: 4 (y_hi: 2, y_lo: 2; y = y_hi * 2 + y_lo), z: 4, core: 2. Of those that a mesh axis runs over, the one named last changes fastest.
Arguments:
- layer_inputs: bfloat16 [2, 16384, 4096], P('section', 'dp'), may hold values from -20 to 20
- norm_gain: float32 [2, 4096], P('section'), may hold values from 0.5 to 1.5
- queries: bfloat16 [2, 16384, 2048], P('section', 'dp'), may hold values from -100 to 100
- output_gradient: bfloat16 [2, 16384, 2048], P('section', 'dp'), may hold values from -6 to 6
- w_key: bfloat16 [2, 4096, 512], P('section'), may hold values from -0.09375 to 0.09375
- value_matrix: bfloat16 [2, 4096, 512], P('section'), may hold values from -0.09375 to 0.09375
- top_grad: bfloat16 [16384, 4096], P('dp'), may hold values from -6 to 6
Outputs:
- key_grad: bfloat16 [2, 4096, 512], P('section')
- value_grad: bfloat16 [2, 4096, 512], P('section')
- input_grad: bfloat16 [2, 16384, 4096], P('section', 'dp')
All inputs are finite; a program needn't handle non-finite values.
Results may differ from a plain program's by a relative error of at most 0.0082.
Values may be sent and summed in bfloat16 or wider, within the bound.
No kernel may reach another device: no remote copies, remote signals or barrier semaphores. Data moves between devices by JAX's collectives and lax.ppermute only.
A program may use at most 128 MiB of HBM per device.

v0:
```python
import jax
import jax.numpy as jnp
from jax import lax
from jax.experimental import pallas as pl
from jax.experimental.pallas import tpu as pltpu
from jax.sharding import Mesh
from jax.sharding import PartitionSpec as P

HEAD = 128
WIDTH = 4096
COLS = 512
ROWS = 256
REPLICAS = 64
LOWER = 128
epsilon = 1e-05
SCALE = HEAD ** (-0.5)


bf16 = jnp.bfloat16
f32 = jnp.float32


def shape(dims, dtype):
    return jax.ShapeDtypeStruct(dims, dtype)


def vmem():
    return pl.BlockSpec(memory_space=pltpu.VMEM)


def held(dims, dtype):
    return pltpu.VMEM(dims, dtype)


def hold(*arrays):
    return tuple(pltpu.with_memory_space_constraint(a, pltpu.VMEM) for a in arrays)


def held(dims, dtype):
    return pltpu.VMEM(dims, dtype)


def hold(*arrays):
    return tuple(pltpu.with_memory_space_constraint(a, pltpu.VMEM) for a in arrays)


def far(*arrays):
    return tuple(pltpu.with_memory_space_constraint(a, pltpu.HBM) for a in arrays)


def budget(mebibytes):
    return pltpu.CompilerParams(vmem_limit_bytes=mebibytes << 20)


def project_body(x, gain, wk, wv, normed, keys, values, inverse, xs, wks, wvs, sems):
    copies = [
        pltpu.make_async_copy(x.at[pl.ds(64 * i, 64), :], xs.at[pl.ds(64 * i, 64), :], sems.at[i])
        for i in range(4)
    ]
    for i in range(8):
        part = pl.ds(512 * i, 512)
        copies.append(pltpu.make_async_copy(wk.at[part, :], wks.at[part, :], sems.at[4 + 2 * i]))
        copies.append(pltpu.make_async_copy(wv.at[part, :], wvs.at[part, :], sems.at[5 + 2 * i]))
    for copy in copies:
        copy.start()
    for i in range(4):
        copies[i].wait()
        rows = slice(64 * i, 64 * i + 64)
        total = jnp.zeros((64, 128), f32)
        for j in range(WIDTH // 128):
            part = xs[rows, j * 128 : (j + 1) * 128].astype(f32)
            total = total + part * part
        mean = jnp.sum(total, axis=1, keepdims=True) / WIDTH
        inverse[rows, :] = jnp.broadcast_to(lax.rsqrt(mean + epsilon), (64, 128))
    inv = inverse[:, :1]
    for i in range(4):
        for copy in copies[4 + 4 * i : 8 + 4 * i]:
            copy.wait()
        part = slice(1024 * i, 1024 * i + 1024)
        low = (xs[:, part].astype(f32) * inv * gain[:, part]).astype(bf16)
        normed[:, part] = low
        part_k = jnp.dot(low, wks[part, :], preferred_element_type=f32)
        part_v = jnp.dot(low, wvs[part, :], preferred_element_type=f32)
        keys[...] = part_k if i == 0 else keys[...] + part_k
        values[...] = part_v if i == 0 else values[...] + part_v


def project(x, gain, wk, wv):
    anywhere = pl.BlockSpec(memory_space=pl.ANY)
    return pl.pallas_call(
        project_body,
        in_specs=[anywhere, vmem(), anywhere, anywhere],
        out_specs=[vmem()] * 7,
        out_shape=[
            held((ROWS, WIDTH), bf16),
            held((ROWS, COLS), f32),
            held((ROWS, COLS), f32),
            held((ROWS, 128), f32),
            held((ROWS, WIDTH), bf16),
            held((WIDTH, COLS), bf16),
            held((WIDTH, COLS), bf16),
        ],
        scratch_shapes=[pltpu.SemaphoreType.DMA((20,))],
        cost_estimate=pl.CostEstimate(flops=2 * ROWS * WIDTH * 1024, bytes_accessed=12 << 20, transcendentals=0),
        name="project",
        compiler_params=budget(16),
    )(*far(x), *hold(gain), *far(wk, wv))


def attend_body(q, og, kf, vf, gk, gv, keep, send, row):
    first_core = lax.axis_index("c") == 0
    nt = (((1,), (1,)), ((), ()))
    key_at = lax.broadcasted_iota(jnp.int32, (HEAD, 512), 0)
    query_at = lax.broadcasted_iota(jnp.int32, (HEAD, 512), 1) & (HEAD - 1)
    causal = key_at <= query_at
    for s in range(2):
        rows = slice(128 * s, 128 * s + 128)
        terms = None
        for j in range(4):
            columns = slice(HEAD * j, HEAD * j + HEAD)

            def heads(ref):
                first = 512 * j
                return jnp.concatenate(
                    [ref[rows, first + h * HEAD : first + (h + 1) * HEAD] for h in range(4)], axis=0
                )

            q4 = heads(q)
            g4 = heads(og)
            key = kf[rows, columns]
            value = vf[rows, columns]
            scores = lax.dot_general(key.astype(bf16), q4, nt, preferred_element_type=f32) * SCALE
            scores = jnp.where(causal, scores, -1e30)
            weight = jnp.exp(scores - jnp.max(scores, axis=0, keepdims=True))
            prob = weight / jnp.sum(weight, axis=0, keepdims=True)
            grad_value = jnp.dot(prob.astype(bf16), g4, preferred_element_type=f32).astype(bf16)
            grad_prob = lax.dot_general(value.astype(bf16), g4, nt, preferred_element_type=f32)
            delta = jnp.sum(prob * grad_prob, axis=0, keepdims=True)
            dscore = (prob * (grad_prob - delta) * SCALE).astype(bf16)
            grad_key = jnp.dot(dscore, q4, preferred_element_type=f32).astype(bf16)
            gk[rows, columns] = grad_key
            gv[rows, columns] = grad_value
            keep[rows, columns] = jnp.where(first_core, grad_value, grad_key)
            send[rows, columns] = jnp.where(first_core, grad_key, grad_value)
            term = grad_key.astype(f32) * key + grad_value.astype(f32) * value
            terms = term if terms is None else terms + term
        row[rows, :] = terms


def attend(q, og, kf, vf):
    return pl.pallas_call(
        attend_body,
        in_specs=[vmem()] * 4,
        out_specs=[vmem()] * 5,
        out_shape=[held((ROWS, COLS), bf16)] * 4 + [held((ROWS, 128), f32)],
        cost_estimate=pl.CostEstimate(flops=600_000_000 * 4, bytes_accessed=4 << 20, transcendentals=1 << 19),
        name="attend",
        compiler_params=budget(8),
    )(*hold(q, og, kf, vf))


def first_index():
    return jnp.where(lax.axis_index("c") == 0, lax.axis_index("x"), lax.axis_index("z"))


def second_index():
    return jnp.where(lax.axis_index("c") == 0, lax.axis_index("z"), lax.axis_index("x"))


def weight_chunk(mine, theirs, grad, grad_theirs, k):
    tn = (((0,), (0,)), ((), ()))
    start = pl.multiple_of(((first_index() + k) % 4) * 1024, 1024)
    part = lax.dot_general(mine[:, pl.ds(start, 1024)], grad[...], tn, preferred_element_type=f32)
    return part + lax.dot_general(
        theirs[:, pl.ds(start, 1024)], grad_theirs[...], tn, preferred_element_type=f32
    )


def weight_far_body(mine, theirs, grad, grad_theirs, top, bottom):
    part = weight_chunk(mine, theirs, grad, grad_theirs, 2).astype(bf16)
    top[...] = part[:512]
    bottom[...] = part[512:]


def weight_far(mine, theirs, grad, grad_theirs):
    return pl.pallas_call(
        weight_far_body,
        in_specs=[vmem()] * 4,
        out_specs=[vmem()] * 2,
        out_shape=[held((512, COLS), bf16)] * 2,
        cost_estimate=pl.CostEstimate(flops=4 * 512 * 512 * 512, bytes_accessed=2 << 20, transcendentals=0),
        name="weight_far",
        compiler_params=budget(8),
    )(*hold(mine, theirs, grad, grad_theirs))


def weight_near_body(mine, theirs, grad, grad_theirs, a_top, a_bottom, b_top, b_bottom):
    part = weight_chunk(mine, theirs, grad, grad_theirs, 1)
    a_top[...] = part[:512]
    a_bottom[...] = part[512:].astype(bf16)
    part = weight_chunk(mine, theirs, grad, grad_theirs, 3)
    b_top[...] = part[:512].astype(bf16)
    b_bottom[...] = part[512:]


def weight_near(mine, theirs, grad, grad_theirs):
    return pl.pallas_call(
        weight_near_body,
        in_specs=[vmem()] * 4,
        out_specs=[vmem()] * 4,
        out_shape=[
            held((512, COLS), f32),
            held((512, COLS), bf16),
            held((512, COLS), bf16),
            held((512, COLS), f32),
        ],
        cost_estimate=pl.CostEstimate(flops=8 * 512 * 512 * 512, bytes_accessed=5 << 20, transcendentals=0),
        name="weight_near",
        compiler_params=budget(12),
    )(*hold(mine, theirs, grad, grad_theirs))


def weight_own_body(mine, theirs, grad, grad_theirs, own):
    own[...] = weight_chunk(mine, theirs, grad, grad_theirs, 0)


def weight_own(mine, theirs, grad, grad_theirs):
    return pl.pallas_call(
        weight_own_body,
        in_specs=[vmem()] * 4,
        out_specs=vmem(),
        out_shape=held((1024, COLS), f32),
        cost_estimate=pl.CostEstimate(flops=4 * 512 * 512 * 512, bytes_accessed=5 << 20, transcendentals=0),
        name="weight_own",
        compiler_params=budget(8),
    )(*hold(mine, theirs, grad, grad_theirs))


def relay_body(own, arrived, out):
    out[...] = (own[...] + arrived[...].astype(f32)).astype(bf16)


def relay(own, arrived):
    return pl.pallas_call(
        relay_body,
        in_specs=[vmem()] * 2,
        out_specs=vmem(),
        out_shape=held((512, COLS), bf16),
        name="relay",
        compiler_params=budget(4),
    )(*hold(own, arrived))


def input_body(gk, gv, wk, wv, x, top, gain, inverse, row, own, lower, upper):
    nt = (((1,), (1,)), ((), ()))
    inv = inverse[:, :1]
    mean = jnp.sum(row[...], axis=1, keepdims=True) * (1.0 / WIDTH)
    factor = inv * inv * mean
    last = lax.axis_index("s") == 1
    for i in range(8):
        tile = slice(512 * i, 512 * i + 512)
        grad_norm = lax.dot_general(gk[...], wk[tile, :], nt, preferred_element_type=f32)
        grad_norm = grad_norm + lax.dot_general(
            gv[...], wv[tile, :], nt, preferred_element_type=f32
        )
        total = inv * (gain[:, tile] * grad_norm) - x[:, tile].astype(f32) * factor
        total = total + jnp.where(last, top[:, tile].astype(f32), 0.0)
        own[:, tile] = total
        low = total.astype(bf16)
        lower[:, tile] = low[:LOWER]
        upper[:, tile] = low[LOWER:]


def input_terms(gk, gv, wk, wv, x, top, gain, inverse, row):
    return pl.pallas_call(
        input_body,
        in_specs=[vmem()] * 9,
        out_specs=[vmem()] * 3,
        out_shape=[held((ROWS, WIDTH), f32), held((LOWER, WIDTH), bf16), held((ROWS - LOWER, WIDTH), bf16)],
        cost_estimate=pl.CostEstimate(flops=2 * ROWS * WIDTH * 1024, bytes_accessed=18 << 20, transcendentals=0),
        name="input_terms",
        compiler_params=budget(8),
    )(*hold(gk, gv, wk, wv, x, top, gain, inverse, row))


def finish_body(own, lower, upper, out, buffer, sems):
    copies = []
    for i in range(ROWS // 32):
        rows = slice(32 * i, 32 * i + 32)
        if 32 * i < LOWER:
            received = lower[rows, :]
        else:
            received = upper[32 * i - LOWER : 32 * i - LOWER + 32, :]
        buffer[rows, :] = (received.astype(f32) + own[rows, :]).astype(bf16)
        part = pl.ds(32 * i, 32)
        copies.append(pltpu.make_async_copy(buffer.at[part, :], out.at[part, :], sems.at[i]))
        copies[-1].start()
    for copy in copies:
        copy.wait()


def finish(own, lower, upper):
    return pl.pallas_call(
        finish_body,
        in_specs=[vmem()] * 3,
        out_specs=pl.BlockSpec(memory_space=pl.ANY),
        out_shape=shape((ROWS, WIDTH), bf16),
        scratch_shapes=[pltpu.VMEM((ROWS, WIDTH), bf16), pltpu.SemaphoreType.DMA((ROWS // 32,))],
        cost_estimate=pl.CostEstimate(flops=ROWS * WIDTH, bytes_accessed=8 << 20, transcendentals=0),
        name="finish",
        compiler_params=budget(8),
    )(*hold(own, lower, upper))


def sum_body(own, b_top, b_bottom, a_top, a_bottom, out, s1, s2, s3, whole):
    whole[:512] = own[:512] + b_top[...].astype(f32) + a_top[...].astype(f32)
    whole[512:] = own[512:] + b_bottom[...].astype(f32) + a_bottom[...].astype(f32)
    for k, ref in ((1, s1), (3, s3), (2, s2), (0, out)):
        rows = pl.ds(pl.multiple_of(((second_index() + k) % 4) * 256, 256), 256)
        ref[...] = whole[rows, :].astype(ref.dtype)


def sum_parts(own, *halves):
    return pl.pallas_call(
        sum_body,
        in_specs=[vmem()] * 5,
        out_specs=[vmem()] * 4,
        out_shape=[held((256, COLS), f32)] + [held((256, COLS), bf16)] * 3,
        scratch_shapes=[pltpu.VMEM((1024, COLS), f32)],
        name="sum_parts",
        compiler_params=budget(8),
    )(*hold(own, *halves))


def total_body(own, r1, r2, r3, out):
    part = own[...] + r1[...].astype(f32) + r2[...].astype(f32)
    out[...] = (part + r3[...].astype(f32)).astype(bf16)


def total(own, received):
    return pl.pallas_call(
        total_body,
        in_specs=[vmem()] * 4,
        out_specs=vmem(),
        out_shape=held((256, COLS), bf16),
        name="total",
        compiler_params=budget(4),
    )(*hold(own, *received))


def mean_body(own, other, out):
    out[...] = ((own[...].astype(f32) + other[...].astype(f32)) / REPLICAS).astype(bf16)


def mean(own, other):
    return pl.pallas_call(
        mean_body,
        in_specs=[vmem()] * 2,
        out_specs=vmem(),
        out_shape=held((256, COLS), bf16),
        name="mean",
        compiler_params=budget(4),
    )(*hold(own, other))


def stack_body(own, r1, r2, r3, top, bottom, whole):
    for k, ref in enumerate((own, r1, r2, r3)):
        rows = pl.ds(pl.multiple_of(((second_index() - k + 4) % 4) * 256, 256), 256)
        whole[rows, :] = ref[...]
    top[...] = whole[:512]
    bottom[...] = whole[512:]


def stack(own, received):
    return pl.pallas_call(
        stack_body,
        in_specs=[vmem()] * 4,
        out_specs=[vmem()] * 2,
        out_shape=[held((512, COLS), bf16)] * 2,
        scratch_shapes=[pltpu.VMEM((1024, COLS), bf16)],
        name="stack",
        compiler_params=budget(4),
    )(*hold(own, *received))


def assemble(entries, start=None):
    count = len(entries)
    extra = 0 if start is None else 2

    def body(*refs):
        core = lax.axis_index("c")
        owners = (lax.axis_index("x"), lax.axis_index("z"))
        pieces = refs[: 2 * count]
        outs = refs[2 * count + extra : 2 * count + extra + 2]
        sems = refs[2 * count + extra + 2]

        def copies(which):
            made = []
            for i, (k, first, own, _) in enumerate(entries):
                for at, gradient in ((2 * i, which), (2 * i + 1, 1 - which)):
                    member = (owners[gradient] - k + 4) % 4
                    rows = pl.ds(pl.multiple_of(member * 1024 + first, 512), own.shape[0])
                    made.append(
                        pltpu.make_async_copy(pieces[at], outs[gradient].at[rows, :], sems.at[at])
                    )
            return made

        for which in (0, 1):

            @pl.when(core == which)
            def _():
                made = copies(which)
                for copy in made:
                    copy.start()
                for copy in made:
                    copy.wait()

    anywhere = pl.BlockSpec(memory_space=pl.ANY)
    blocks = [block for entry in entries for block in entry[2:]]
    return pl.pallas_call(
        body,
        in_specs=[vmem()] * (2 * count) + [anywhere] * extra,
        out_specs=[anywhere] * 2,
        out_shape=[shape((WIDTH, COLS), bf16)] * 2,
        scratch_shapes=[pltpu.SemaphoreType.DMA((2 * count,))],
        input_output_aliases={} if start is None else {2 * count: 0, 2 * count + 1: 1},
        name="assemble",
        compiler_params=budget(4),
    )(*hold(*blocks), *(() if start is None else start))


def swap(value, axis):
    return lax.ppermute(value, axis, [(0, 1), (1, 0)])


def ring(value, stage, steps):
    pairs = []
    for z in range(4):
        for x in range(4):
            for c in range(2):
                along_x = (c == 0) == (stage == 1)
                to = (z, (x + steps) % 4) if along_x else ((z + steps) % 4, x)
                pairs.append(((z * 4 + x) * 2 + c, (to[0] * 4 + to[1]) * 2 + c))
    return lax.ppermute(value, ("z", "x", "c"), pairs)


def down(value):
    return lax.ppermute(value, "s", [(1, 0)])


def send_all(sends, stage):
    got = [None] * 3
    for k in (1, 3, 2):
        got[k - 1] = ring(sends[k - 1], stage, k)
    return got


def all_steps(layer_inputs, norm_gain, queries, output_gradient, w_key, value_matrix, top_grad):
    x, wk, wv = layer_inputs[0], w_key[0], value_matrix[0]
    normed, keys, values, inverse, x, wk, wv = project(x, norm_gain, wk, wv)
    theirs = swap(normed, "c")
    gk, gv, keep, send, row = attend(queries[0], output_gradient[0], keys, values)
    operands = (normed, theirs, keep, swap(send, "c"))
    top, bottom = weight_far(*operands)
    top, bottom = ring(top, 1, 1), ring(bottom, 1, 3)
    a_top, a_bottom, b_top, b_bottom = weight_near(*operands)
    from_bottom, from_top = ring(a_bottom, 1, 1), ring(b_top, 1, 3)
    kept = weight_own(*operands)
    a_top, b_bottom = relay(a_top, top), relay(b_bottom, bottom)
    halves = (ring(a_top, 1, 1), from_bottom, from_top, ring(b_bottom, 1, 3))
    own, lower, upper = input_terms(gk, gv, wk, wv, x, top_grad, norm_gain, inverse, row)
    lower_got = down(lower)
    kept, *sends = sum_parts(kept, *halves)
    got = send_all(sends, 2)
    part = total(kept, got)
    block = mean(part, swap(part, "y"))
    upper_got = down(upper)
    got = send_all([block] * 3, 2)
    top, bottom = stack(block, got)
    behind_top, ahead_bottom = ring(top, 1, 1), ring(bottom, 1, 3)
    behind_bottom, ahead_top = ring(bottom, 1, 1), ring(top, 1, 3)
    blocks = (
        (0, 0, top),
        (0, 512, bottom),
        (1, 0, behind_top),
        (3, 512, ahead_bottom),
        (1, 512, behind_bottom),
        (3, 0, ahead_top),
        (2, 0, ring(behind_top, 1, 1)),
        (2, 512, ring(ahead_bottom, 1, 3)),
    )
    entries = [(k, first, block, swap(block, "c")) for k, first, block in blocks]
    part = assemble(entries[:2])
    part = assemble(entries[2:4], part)
    part = assemble(entries[4:6], part)
    value_grad, key_grad = assemble(entries[6:], part)
    input_grad = finish(own, lower_got, upper_got)
    return (key_grad[None], value_grad[None], input_grad[None])


def solution(mesh):
    wide = Mesh(mesh.devices.reshape(2, 4, 4, 2, 2), ("s", "z", "x", "y", "c"))
    dp = ("z", "x", "y", "c")
    in_specs = (
        P("s", dp, None),
        P("s", None),
        P("s", dp, None),
        P("s", dp, None),
        P("s", None, None),
        P("s", None, None),
        P(dp, None),
    )
    out_specs = (P("s", None, None), P("s", None, None), P("s", dp, None))
    return jax.shard_map(all_steps, mesh=wide, in_specs=in_specs, out_specs=out_specs, check_vma=False)
```

profile of v0, /device:TPU:1, one launch (start us, length us, event | category | flops | bytes accessed | tf_op | source)
XLA Modules:
  0.0 111.1 jit_solution(6671403819256961015)
XLA Ops:
  1.4 5.1 %project.1 = (bf16[256,4096]{1,0:T(8,128)(2,1)S(1)}, f32[256,512]{1,0:T(8,128)S(1)}, f32[256,512]{1,0:T(8,128)S(1)}, f32[256,128]{1,0:T(8,128)S(1)}, bf16[256,40...) custom-call(bf16[256,4096]{1,0:T(8,128)(2,1)} %bitcast.14, ...), custom_call_target="tpu_custom_call" | custom-call | flops 2147483648 | bytes 12582912 | tf_op jit(solution)/shard_map/project/pallas_call | solution.py:90
  6.4 1.5 %collective-permute-start = (bf16[256,4096]{1,0:T(8,128)(2,1)S(1)}, bf16[256,4096]{1,0:T(8,128)(2,1)S(1)}, u32[]{:S(2)}, u32[]{:S(2)}) collective-permute-start(bf16[256,4096]{1,0:T(8,128)(2,1)S(1)} %get-tuple-element.38.mine), channel_id=1, source_target_pairs={{0,1},{1,0},{2,3},{3,2},{4,5},{5,4},{6,7},{7,6},{8,9},{9,8},{10,11... | collective-permute-start | bytes 6291464 | tf_op jit(solution)/shard_map/ppermute | solution.py:433
  7.9 4.0 %attend.1 = (bf16[256,512]{1,0:T(8,128)(2,1)S(1)}, bf16[256,512]{1,0:T(8,128)(2,1)S(1)}, bf16[256,512]{1,0:T(8,128)(2,1)S(1)}, bf16[256,512]{1,0:T(8,128)(2,1)S(1)}, f32[256,128]{1,0:T(8,128)S(1)}) custom-call(bf16[256,2048]{1,0:T(8,128)(2,1)S(1)} %bitcast.8, bf16[256,2048]{1,0:T(8,128)(2,1)S(1)} %bitcast.9, f32[256,512]{1,0:T(8,128)S(1)} %get-tuple-element.39.kf, ...), custom_call_target="tpu_custom_call" | custom-call | flops 2400000000 | bytes 4194304 | tf_op jit(solution)/shard_map/attend/pallas_call | solution.py:151
  12.0 1.5 %collective-permute-done.1.grad_theirs = bf16[256,512]{1,0:T(8,128)(2,1)S(1)} collective-permute-done((bf16[256,512]{1,0:T(8,128)(2,1)S(1)}, bf16[256,512]{1,0:T(8,128)(2,1)S(1)}, u32[]{:S(2)}, u32[]{:S(2)}) %collective-permute-start.1) | collective-permute-done | bytes 262176 | tf_op jit(solution)/shard_map/ppermute | solution.py:433
  14.3 3.9 %collective-permute-start.6 = (bf16[512,512]{1,0:T(8,128)(2,1)S(1)}, bf16[512,512]{1,0:T(8,128)(2,1)S(1)}, u32[]{:S(2)}, u32[]{:S(2)}) collective-permute-start(bf16[512,512]{1,0:T(8,128)(2,1)S(1)} %get-tuple-element.48), channel_id=1, source_target_pairs={{0,12},{1,49},{4,0},{5,53},{8,4},{9,57},{12,8},{13,61},{16,28},{17... | collective-permute-start | bytes 1572872 | tf_op jit(solution)/shard_map/ppermute | solution.py:444
  19.6 2.7 %collective-permute-start.5 = (bf16[512,512]{1,0:T(8,128)(2,1)S(1)}, bf16[512,512]{1,0:T(8,128)(2,1)S(1)}, u32[]{:S(2)}, u32[]{:S(2)}) collective-permute-start(bf16[512,512]{1,0:T(8,128)(2,1)S(1)} %get-tuple-element.46), channel_id=1, source_target_pairs={{0,12},{1,49},{4,0},{5,53},{8,4},{9,57},{12,8},{13,61},{16,28},{17... | collective-permute-start | bytes 1572872 | tf_op jit(solution)/shard_map/ppermute | solution.py:444
  22.4 2.0 %collective-permute-done.6.arrived = bf16[512,512]{1,0:T(8,128)(2,1)S(1)} collective-permute-done((bf16[512,512]{1,0:T(8,128)(2,1)S(1)}, bf16[512,512]{1,0:T(8,128)(2,1)S(1)}, u32[]{:S(2)}, u32[]{:S(2)}) %collective-permute-start.6) | collective-permute-done | bytes 524320 | tf_op jit(solution)/shard_map/ppermute | solution.py:444
  24.5 3.5 %collective-permute-start.7 = (bf16[512,512]{1,0:T(8,128)(2,1)S(1)}, bf16[512,512]{1,0:T(8,128)(2,1)S(1)}, u32[]{:S(2)}, u32[]{:S(2)}) collective-permute-start(bf16[512,512]{1,0:T(8,128)(2,1)S(1)} %relay.3), channel_id=1, source_target_pairs={{0,12},{1,49},{4,0},{5,53},{8,4},{9,57},{12,8},{13,61},{16,28},{17... | collective-permute-start | bytes 1572872 | tf_op jit(solution)/shard_map/ppermute | solution.py:444
  28.3 2.6 %input_terms.1 = (f32[256,4096]{1,0:T(8,128)S(1)}, bf16[128,4096]{1,0:T(8,128)(2,1)S(1)}, bf16[128,4096]{1,0:T(8,128)(2,1)S(1)}) custom-call(bf16[256,512]{1,0:T(8,128)(2,1)S(1)} %get-tuple-element.63.gk, bf16[256,512]{1,0:T(8,128)(2,1)S(1)} %get-tuple-element.64.gv, bf16[4096,512]{1,0:T(8,128)(2,1)S(1)} %get-tuple-element.65.wk, ...), custom_call_target="tpu_custom_call" | custom-call | flops 2147483648 | bytes 18874368 | tf_op jit(solution)/shard_map/input_terms/pallas_call | solution.py:275
  33.4 2.2 %collective-permute-done.7.a_bottom = bf16[512,512]{1,0:T(8,128)(2,1)S(1)} collective-permute-done((bf16[512,512]{1,0:T(8,128)(2,1)S(1)}, bf16[512,512]{1,0:T(8,128)(2,1)S(1)}, u32[]{:S(2)}, u32[]{:S(2)}) %collective-permute-start.7) | collective-permute-done | bytes 524320 | tf_op jit(solution)/shard_map/ppermute | solution.py:444
  35.6 3.4 %collective-permute-done.3.b_top = bf16[512,512]{1,0:T(8,128)(2,1)S(1)} collective-permute-done((bf16[512,512]{1,0:T(8,128)(2,1)S(1)}, bf16[512,512]{1,0:T(8,128)(2,1)S(1)}, u32[]{:S(2)}, u32[]{:S(2)}) %collective-permute-start.3) | collective-permute-done | bytes 524320 | tf_op jit(solution)/shard_map/ppermute | solution.py:444
  39.6 2.6 %collective-permute-start.10 = (bf16[256,512]{1,0:T(8,128)(2,1)S(1)}, bf16[256,512]{1,0:T(8,128)(2,1)S(1)}, u32[]{:S(2)}, u32[]{:S(2)}) collective-permute-start(bf16[256,512]{1,0:T(8,128)(2,1)S(1)} %get-tuple-element.52), channel_id=1, source_target_pairs={{0,48},{1,13},{4,52},{5,1},{8,56},{9,5},{12,60},{13,9},{16,0},{17,... | collective-permute-start | bytes 786440 | tf_op jit(solution)/shard_map/ppermute | solution.py:444
  42.1 1.7 %collective-permute-start.9 = (bf16[256,512]{1,0:T(8,128)(2,1)S(1)}, bf16[256,512]{1,0:T(8,128)(2,1)S(1)}, u32[]{:S(2)}, u32[]{:S(2)}) collective-permute-start(bf16[256,512]{1,0:T(8,128)(2,1)S(1)} %get-tuple-element.51), channel_id=1, source_target_pairs={{0,32},{1,9},{4,36},{5,13},{8,40},{9,1},{12,44},{13,5},{16,48},{17... | collective-permute-start | bytes 786440 | tf_op jit(solution)/shard_map/ppermute | solution.py:444
  43.9 1.6 %collective-permute-done.10.r3 = bf16[256,512]{1,0:T(8,128)(2,1)S(1)} collective-permute-done((bf16[256,512]{1,0:T(8,128)(2,1)S(1)}, bf16[256,512]{1,0:T(8,128)(2,1)S(1)}, u32[]{:S(2)}, u32[]{:S(2)}) %collective-permute-start.10) | collective-permute-done | bytes 262176 | tf_op jit(solution)/shard_map/ppermute | solution.py:444
  45.5 6.2 %collective-permute-done.8.r1 = bf16[256,512]{1,0:T(8,128)(2,1)S(1)} collective-permute-done((bf16[256,512]{1,0:T(8,128)(2,1)S(1)}, bf16[256,512]{1,0:T(8,128)(2,1)S(1)}, u32[]{:S(2)}, u32[]{:S(2)}) %collective-permute-start.8) | collective-permute-done | bytes 262176 | tf_op jit(solution)/shard_map/ppermute | solution.py:444
  54.3 3.1 %collective-permute-done.11.other = bf16[256,512]{1,0:T(8,128)(2,1)S(1)} collective-permute-done((bf16[256,512]{1,0:T(8,128)(2,1)S(1)}, bf16[256,512]{1,0:T(8,128)(2,1)S(1)}, u32[]{:S(2)}, u32[]{:S(2)}) %collective-permute-start.11) | collective-permute-done | bytes 262176 | tf_op jit(solution)/shard_map/ppermute | solution.py:433
  57.6 1.7 %collective-permute-start.13 = (bf16[256,512]{1,0:T(8,128)(2,1)S(1)}, bf16[256,512]{1,0:T(8,128)(2,1)S(1)}, u32[]{:S(2)}, u32[]{:S(2)}) collective-permute-start(bf16[256,512]{1,0:T(8,128)(2,1)S(1)} %mean.1.own), channel_id=1, source_target_pairs={{0,32},{1,9},{4,36},{5,13},{8,40},{9,1},{12,44},{13,5},{16,48},{17... | collective-permute-start | bytes 786440 | tf_op jit(solution)/shard_map/ppermute | solution.py:444
  59.3 1.6 %collective-permute-start.14 = (bf16[256,512]{1,0:T(8,128)(2,1)S(1)}, bf16[256,512]{1,0:T(8,128)(2,1)S(1)}, u32[]{:S(2)}, u32[]{:S(2)}) collective-permute-start(bf16[256,512]{1,0:T(8,128)(2,1)S(1)} %mean.1.own), channel_id=1, source_target_pairs={{0,48},{1,13},{4,52},{5,1},{8,56},{9,5},{12,60},{13,9},{16,0},{17,... | collective-permute-start | bytes 786440 | tf_op jit(solution)/shard_map/ppermute | solution.py:444
  60.8 6.3 %collective-permute-done.12.r1 = bf16[256,512]{1,0:T(8,128)(2,1)S(1)} collective-permute-done((bf16[256,512]{1,0:T(8,128)(2,1)S(1)}, bf16[256,512]{1,0:T(8,128)(2,1)S(1)}, u32[]{:S(2)}, u32[]{:S(2)}) %collective-permute-start.12) | collective-permute-done | bytes 262176 | tf_op jit(solution)/shard_map/ppermute | solution.py:444
  67.9 4.5 %collective-permute-start.27 = (bf16[512,512]{1,0:T(8,128)(2,1)S(1)}, bf16[512,512]{1,0:T(8,128)(2,1)S(1)}, u32[]{:S(2)}, u32[]{:S(2)}) collective-permute-start(bf16[512,512]{1,0:T(8,128)(2,1)S(1)} %get-tuple-element.53.refs_0_), channel_id=1, source_target_pairs={{0,1},{1,0},{2,3},{3,2},{4,5},{5,4},{6,7},{7,6},{8,9},{9,8},{10,11... | collective-permute-start | bytes 1572872 | tf_op jit(solution)/shard_map/ppermute | solution.py:433
  72.5 2.5 %collective-permute-start.18 = (bf16[512,512]{1,0:T(8,128)(2,1)S(1)}, bf16[512,512]{1,0:T(8,128)(2,1)S(1)}, u32[]{:S(2)}, u32[]{:S(2)}) collective-permute-start(bf16[512,512]{1,0:T(8,128)(2,1)S(1)} %get-tuple-element.54.refs_2_), channel_id=1, source_target_pairs={{0,12},{1,49},{4,0},{5,53},{8,4},{9,57},{12,8},{13,61},{16,28},{17... | collective-permute-start | bytes 1572872 | tf_op jit(solution)/shard_map/ppermute | solution.py:444
  75.0 12.1 %collective-permute-done.30.upper = bf16[128,4096]{1,0:T(8,128)(2,1)S(1)} collective-permute-done((bf16[128,4096]{1,0:T(8,128)(2,1)S(1)}, bf16[128,4096]{1,0:T(8,128)(2,1)S(1)}, u32[]{:S(2)}, u32[]{:S(2)}) %collective-permute-start.30) | collective-permute-done | bytes 1048608 | tf_op jit(solution)/shard_map/ppermute | solution.py:448
  87.1 2.7 %collective-permute-start.23 = (bf16[512,512]{1,0:T(8,128)(2,1)S(1)}, bf16[512,512]{1,0:T(8,128)(2,1)S(1)}, u32[]{:S(2)}, u32[]{:S(2)}) collective-permute-start(bf16[512,512]{1,0:T(8,128)(2,1)S(1)} %get-tuple-element.53.refs_0_), channel_id=1, source_target_pairs={{0,12},{1,49},{4,0},{5,53},{8,4},{9,57},{12,8},{13,61},{16,28},{17... | collective-permute-start | bytes 1572872 | tf_op jit(solution)/shard_map/ppermute | solution.py:444
  89.8 1.4 %collective-permute-start.25 = (bf16[512,512]{1,0:T(8,128)(2,1)S(1)}, bf16[512,512]{1,0:T(8,128)(2,1)S(1)}, u32[]{:S(2)}, u32[]{:S(2)}) collective-permute-start(bf16[512,512]{1,0:T(8,128)(2,1)S(1)} %collective-permute-done.15.refs_0_), channel_id=1, source_target_pairs={{0,1},{1,0},{2,3},{3,2},{4,5},{5,4},{6,7},{7,6},{8,9},{9,8},{10,11... | collective-permute-start | bytes 1572872 | tf_op jit(solution)/shard_map/ppermute | solution.py:433
  91.2 2.7 %collective-permute-start.19 = (bf16[512,512]{1,0:T(8,128)(2,1)S(1)}, bf16[512,512]{1,0:T(8,128)(2,1)S(1)}, u32[]{:S(2)}, u32[]{:S(2)}) collective-permute-start(bf16[512,512]{1,0:T(8,128)(2,1)S(1)} %collective-permute-done.18.refs_2_), channel_id=1, source_target_pairs={{0,12},{1,49},{4,0},{5,53},{8,4},{9,57},{12,8},{13,61},{16,28},{17... | collective-permute-start | bytes 1572872 | tf_op jit(solution)/shard_map/ppermute | solution.py:444
  93.9 2.7 %collective-permute-done.21.refs_0_ = bf16[512,512]{1,0:T(8,128)(2,1)S(1)} collective-permute-done((bf16[512,512]{1,0:T(8,128)(2,1)S(1)}, bf16[512,512]{1,0:T(8,128)(2,1)S(1)}, u32[]{:S(2)}, u32[]{:S(2)}) %collective-permute-start.21) | collective-permute-done | bytes 524320 | tf_op jit(solution)/shard_map/ppermute | solution.py:444
  96.6 1.7 %collective-permute-start.26 = (bf16[512,512]{1,0:T(8,128)(2,1)S(1)}, bf16[512,512]{1,0:T(8,128)(2,1)S(1)}, u32[]{:S(2)}, u32[]{:S(2)}) collective-permute-start(bf16[512,512]{1,0:T(8,128)(2,1)S(1)} %collective-permute-done.18.refs_2_), channel_id=1, source_target_pairs={{0,1},{1,0},{2,3},{3,2},{4,5},{5,4},{6,7},{7,6},{8,9},{9,8},{10,11... | collective-permute-start | bytes 1572872 | tf_op jit(solution)/shard_map/ppermute | solution.py:433
  98.9 3.4 %collective-permute-done.16.refs_0_ = bf16[512,512]{1,0:T(8,128)(2,1)S(1)} collective-permute-done((bf16[512,512]{1,0:T(8,128)(2,1)S(1)}, bf16[512,512]{1,0:T(8,128)(2,1)S(1)}, u32[]{:S(2)}, u32[]{:S(2)}) %collective-permute-start.16) | collective-permute-done | bytes 524320 | tf_op jit(solution)/shard_map/ppermute | solution.py:444
  102.2 1.7 %collective-permute-start.17 = (bf16[512,512]{1,0:T(8,128)(2,1)S(1)}, bf16[512,512]{1,0:T(8,128)(2,1)S(1)}, u32[]{:S(2)}, u32[]{:S(2)}) collective-permute-start(bf16[512,512]{1,0:T(8,128)(2,1)S(1)} %collective-permute-done.16.refs_0_), channel_id=1, source_target_pairs={{0,1},{1,0},{2,3},{3,2},{4,5},{5,4},{6,7},{7,6},{8,9},{9,8},{10,11... | collective-permute-start | bytes 1572872 | tf_op jit(solution)/shard_map/ppermute | solution.py:433
  104.0 1.4 %finish.1 = bf16[256,4096]{1,0:T(8,128)(2,1)} custom-call(f32[256,4096]{1,0:T(8,128)S(1)} %get-tuple-element.70.own, bf16[128,4096]{1,0:T(8,128)(2,1)S(1)} %collective-permute-done.29.lower, bf16[128,4096]{1,0:T(8,128)(2,1)S(1)} %collective-permute-done.30.upper), custom_call_target="tpu_custom_call" | custom-call | flops 1048576 | bytes 8388608 | tf_op jit(solution)/shard_map/finish/pallas_call | solution.py:303
  106.8 1.4 %assemble.5 = (bf16[4096,512]{1,0:T(8,128)(2,1)}, bf16[4096,512]{1,0:T(8,128)(2,1)}) custom-call(bf16[512,512]{1,0:T(8,128)(2,1)S(1)} %collective-permute-done.15.refs_0_, bf16[512,512]{1,0:T(8,128)(2,1)S(1)} %collective-permute-done.25.refs_1_, bf16[512,512]{1,0:T(8,128)(2,1)S(1)} %collective-permute-done.18.refs_2_, ...), custom_call_target="tpu_custom_call", output_to_operand_aliasing={{0}: (4, {}), {1}: (5, {})} | custom-call | tf_op jit(solution)/shard_map/assemble/pallas_call | solution.py:420
  108.2 1.4 %assemble.6 = (bf16[4096,512]{1,0:T(8,128)(2,1)}, bf16[4096,512]{1,0:T(8,128)(2,1)}) custom-call(bf16[512,512]{1,0:T(8,128)(2,1)S(1)} %collective-permute-done.21.refs_0_, bf16[512,512]{1,0:T(8,128)(2,1)S(1)} %collective-permute-done.22.refs_1_, bf16[512,512]{1,0:T(8,128)(2,1)S(1)} %collective-permute-done.23.refs_2_, ...), custom_call_target="tpu_custom_call", output_to_operand_aliasing={{0}: (4, {}), {1}: (5, {})} | custom-call | tf_op jit(solution)/shard_map/assemble/pallas_call | solution.py:420
  (57 shorter events, 13.5 us)
Async XLA Ops:
  6.4 7.1 %collective-permute-start = (bf16[256,4096]{1,0:T(8,128)(2,1)S(1)}, bf16[256,4096]{1,0:T(8,128)(2,1)S(1)}, u32[]{:S(2)}, u32[]{:S(2)}) collective-permute-start(bf16[256,4096]{1,0:T(8,128)(2,1)S(1)} %get-tuple-element.38.mine), channel_id=1, source_target_pairs={{0,1},{1,0},{2,3},{3,2},{4,5},{5,4},{6,7},{7,6},{8,9},{9,8},{10,11... | collective-permute-start | bytes 6291464 | tf_op jit(solution)/shard_map/ppermute | solution.py:433
  11.9 1.6 %collective-permute-start.1 = (bf16[256,512]{1,0:T(8,128)(2,1)S(1)}, bf16[256,512]{1,0:T(8,128)(2,1)S(1)}, u32[]{:S(2)}, u32[]{:S(2)}) collective-permute-start(bf16[256,512]{1,0:T(8,128)(2,1)S(1)} %get-tuple-element.42), channel_id=1, source_target_pairs={{0,1},{1,0},{2,3},{3,2},{4,5},{5,4},{6,7},{7,6},{8,9},{9,8},{10,11... | collective-permute-start | bytes 786440 | tf_op jit(solution)/shard_map/ppermute | solution.py:433
  14.3 10.1 %collective-permute-start.6 = (bf16[512,512]{1,0:T(8,128)(2,1)S(1)}, bf16[512,512]{1,0:T(8,128)(2,1)S(1)}, u32[]{:S(2)}, u32[]{:S(2)}) collective-permute-start(bf16[512,512]{1,0:T(8,128)(2,1)S(1)} %get-tuple-element.48), channel_id=1, source_target_pairs={{0,12},{1,49},{4,0},{5,53},{8,4},{9,57},{12,8},{13,61},{16,28},{17... | collective-permute-start | bytes 1572872 | tf_op jit(solution)/shard_map/ppermute | solution.py:444
  18.2 10.1 %copy-start.2 = (f32[1,4096]{1,0:T(1,128)S(1)}, f32[1,4096]{1,0:T(1,128)}, u32[]{:S(2)}) copy-start(f32[1,4096]{1,0:T(1,128)} %gain.3) | copy-start | bytes 49156
  18.2 9.7 %collective-permute-start.2 = (bf16[512,512]{1,0:T(8,128)(2,1)S(1)}, bf16[512,512]{1,0:T(8,128)(2,1)S(1)}, u32[]{:S(2)}, u32[]{:S(2)}) collective-permute-start(bf16[512,512]{1,0:T(8,128)(2,1)S(1)} %get-tuple-element.44), channel_id=1, source_target_pairs={{0,4},{1,17},{4,8},{5,21},{8,12},{9,25},{12,0},{13,29},{16,20},{17... | collective-permute-start | bytes 1572872 | tf_op jit(solution)/shard_map/ppermute | solution.py:444
  19.6 13.8 %collective-permute-start.4 = (bf16[512,512]{1,0:T(8,128)(2,1)S(1)}, bf16[512,512]{1,0:T(8,128)(2,1)S(1)}, u32[]{:S(2)}, u32[]{:S(2)}) collective-permute-start(bf16[512,512]{1,0:T(8,128)(2,1)S(1)} %get-tuple-element.45), channel_id=1, source_target_pairs={{0,4},{1,17},{4,8},{5,21},{8,12},{9,25},{12,0},{13,29},{16,20},{17... | collective-permute-start | bytes 1572872 | tf_op jit(solution)/shard_map/ppermute | solution.py:444
  19.6 13.8 %collective-permute-start.5 = (bf16[512,512]{1,0:T(8,128)(2,1)S(1)}, bf16[512,512]{1,0:T(8,128)(2,1)S(1)}, u32[]{:S(2)}, u32[]{:S(2)}) collective-permute-start(bf16[512,512]{1,0:T(8,128)(2,1)S(1)} %get-tuple-element.46), channel_id=1, source_target_pairs={{0,12},{1,49},{4,0},{5,53},{8,4},{9,57},{12,8},{13,61},{16,28},{17... | collective-permute-start | bytes 1572872 | tf_op jit(solution)/shard_map/ppermute | solution.py:444
  24.5 11.1 %collective-permute-start.7 = (bf16[512,512]{1,0:T(8,128)(2,1)S(1)}, bf16[512,512]{1,0:T(8,128)(2,1)S(1)}, u32[]{:S(2)}, u32[]{:S(2)}) collective-permute-start(bf16[512,512]{1,0:T(8,128)(2,1)S(1)} %relay.3), channel_id=1, source_target_pairs={{0,12},{1,49},{4,0},{5,53},{8,4},{9,57},{12,8},{13,61},{16,28},{17... | collective-permute-start | bytes 1572872 | tf_op jit(solution)/shard_map/ppermute | solution.py:444
  28.0 11.0 %collective-permute-start.3 = (bf16[512,512]{1,0:T(8,128)(2,1)S(1)}, bf16[512,512]{1,0:T(8,128)(2,1)S(1)}, u32[]{:S(2)}, u32[]{:S(2)}) collective-permute-start(bf16[512,512]{1,0:T(8,128)(2,1)S(1)} %relay.2), channel_id=1, source_target_pairs={{0,4},{1,17},{4,8},{5,21},{8,12},{9,25},{12,0},{13,29},{16,20},{17... | collective-permute-start | bytes 1572872 | tf_op jit(solution)/shard_map/ppermute | solution.py:444
  30.9 41.6 %collective-permute-start.29 = (bf16[128,4096]{1,0:T(8,128)(2,1)S(1)}, bf16[128,4096]{1,0:T(8,128)(2,1)S(1)}, u32[]{:S(2)}, u32[]{:S(2)}) collective-permute-start(bf16[128,4096]{1,0:T(8,128)(2,1)S(1)} %get-tuple-element.71), channel_id=1, source_target_pairs={{64,0},{65,1},{66,2},{67,3},{68,4},{69,5},{70,6},{71,7},{72,8},{73... | collective-permute-start | bytes 3145736 | tf_op jit(solution)/shard_map/ppermute | solution.py:448
  39.6 5.9 %collective-permute-start.10 = (bf16[256,512]{1,0:T(8,128)(2,1)S(1)}, bf16[256,512]{1,0:T(8,128)(2,1)S(1)}, u32[]{:S(2)}, u32[]{:S(2)}) collective-permute-start(bf16[256,512]{1,0:T(8,128)(2,1)S(1)} %get-tuple-element.52), channel_id=1, source_target_pairs={{0,48},{1,13},{4,52},{5,1},{8,56},{9,5},{12,60},{13,9},{16,0},{17,... | collective-permute-start | bytes 786440 | tf_op jit(solution)/shard_map/ppermute | solution.py:444
  42.1 9.5 %collective-permute-start.8 = (bf16[256,512]{1,0:T(8,128)(2,1)S(1)}, bf16[256,512]{1,0:T(8,128)(2,1)S(1)}, u32[]{:S(2)}, u32[]{:S(2)}) collective-permute-start(bf16[256,512]{1,0:T(8,128)(2,1)S(1)} %get-tuple-element.50), channel_id=1, source_target_pairs={{0,16},{1,5},{4,20},{5,9},{8,24},{9,13},{12,28},{13,1},{16,32},{17... | collective-permute-start | bytes 786440 | tf_op jit(solution)/shard_map/ppermute | solution.py:444
  42.1 9.5 %collective-permute-start.9 = (bf16[256,512]{1,0:T(8,128)(2,1)S(1)}, bf16[256,512]{1,0:T(8,128)(2,1)S(1)}, u32[]{:S(2)}, u32[]{:S(2)}) collective-permute-start(bf16[256,512]{1,0:T(8,128)(2,1)S(1)} %get-tuple-element.51), channel_id=1, source_target_pairs={{0,32},{1,9},{4,36},{5,13},{8,40},{9,1},{12,44},{13,5},{16,48},{17... | collective-permute-start | bytes 786440 | tf_op jit(solution)/shard_map/ppermute | solution.py:444
  51.8 5.6 %collective-permute-start.11 = (bf16[256,512]{1,0:T(8,128)(2,1)S(1)}, bf16[256,512]{1,0:T(8,128)(2,1)S(1)}, u32[]{:S(2)}, u32[]{:S(2)}) collective-permute-start(bf16[256,512]{1,0:T(8,128)(2,1)S(1)} %total.1.own), channel_id=1, source_target_pairs={{0,2},{2,0},{1,3},{3,1},{4,6},{6,4},{5,7},{7,5},{8,10},{10,8},{9,1... | collective-permute-start | bytes 786440 | tf_op jit(solution)/shard_map/ppermute | solution.py:433
  53.0 34.1 %collective-permute-start.30 = (bf16[128,4096]{1,0:T(8,128)(2,1)S(1)}, bf16[128,4096]{1,0:T(8,128)(2,1)S(1)}, u32[]{:S(2)}, u32[]{:S(2)}) collective-permute-start(bf16[128,4096]{1,0:T(8,128)(2,1)S(1)} %get-tuple-element.72), channel_id=1, source_target_pairs={{64,0},{65,1},{66,2},{67,3},{68,4},{69,5},{70,6},{71,7},{72,8},{73... | collective-permute-start | bytes 3145736 | tf_op jit(solution)/shard_map/ppermute | solution.py:448
  57.5 9.6 %collective-permute-start.12 = (bf16[256,512]{1,0:T(8,128)(2,1)S(1)}, bf16[256,512]{1,0:T(8,128)(2,1)S(1)}, u32[]{:S(2)}, u32[]{:S(2)}) collective-permute-start(bf16[256,512]{1,0:T(8,128)(2,1)S(1)} %mean.1.own), channel_id=1, source_target_pairs={{0,16},{1,5},{4,20},{5,9},{8,24},{9,13},{12,28},{13,1},{16,32},{17... | collective-permute-start | bytes 786440 | tf_op jit(solution)/shard_map/ppermute | solution.py:444
  57.6 9.5 %collective-permute-start.13 = (bf16[256,512]{1,0:T(8,128)(2,1)S(1)}, bf16[256,512]{1,0:T(8,128)(2,1)S(1)}, u32[]{:S(2)}, u32[]{:S(2)}) collective-permute-start(bf16[256,512]{1,0:T(8,128)(2,1)S(1)} %mean.1.own), channel_id=1, source_target_pairs={{0,32},{1,9},{4,36},{5,13},{8,40},{9,1},{12,44},{13,5},{16,48},{17... | collective-permute-start | bytes 786440 | tf_op jit(solution)/shard_map/ppermute | solution.py:444
  59.3 8.4 %collective-permute-start.14 = (bf16[256,512]{1,0:T(8,128)(2,1)S(1)}, bf16[256,512]{1,0:T(8,128)(2,1)S(1)}, u32[]{:S(2)}, u32[]{:S(2)}) collective-permute-start(bf16[256,512]{1,0:T(8,128)(2,1)S(1)} %mean.1.own), channel_id=1, source_target_pairs={{0,48},{1,13},{4,52},{5,1},{8,56},{9,5},{12,60},{13,9},{16,0},{17,... | collective-permute-start | bytes 786440 | tf_op jit(solution)/shard_map/ppermute | solution.py:444
  67.9 19.2 %collective-permute-start.27 = (bf16[512,512]{1,0:T(8,128)(2,1)S(1)}, bf16[512,512]{1,0:T(8,128)(2,1)S(1)}, u32[]{:S(2)}, u32[]{:S(2)}) collective-permute-start(bf16[512,512]{1,0:T(8,128)(2,1)S(1)} %get-tuple-element.53.refs_0_), channel_id=1, source_target_pairs={{0,1},{1,0},{2,3},{3,2},{4,5},{5,4},{6,7},{7,6},{8,9},{9,8},{10,11... | collective-permute-start | bytes 1572872 | tf_op jit(solution)/shard_map/ppermute | solution.py:433
  72.4 17.4 %collective-permute-start.15 = (bf16[512,512]{1,0:T(8,128)(2,1)S(1)}, bf16[512,512]{1,0:T(8,128)(2,1)S(1)}, u32[]{:S(2)}, u32[]{:S(2)}) collective-permute-start(bf16[512,512]{1,0:T(8,128)(2,1)S(1)} %get-tuple-element.53.refs_0_), channel_id=1, source_target_pairs={{0,4},{1,17},{4,8},{5,21},{8,12},{9,25},{12,0},{13,29},{16,20},{17... | collective-permute-start | bytes 1572872 | tf_op jit(solution)/shard_map/ppermute | solution.py:444
  72.4 18.8 %collective-permute-start.28 = (bf16[512,512]{1,0:T(8,128)(2,1)S(1)}, bf16[512,512]{1,0:T(8,128)(2,1)S(1)}, u32[]{:S(2)}, u32[]{:S(2)}) collective-permute-start(bf16[512,512]{1,0:T(8,128)(2,1)S(1)} %get-tuple-element.54.refs_2_), channel_id=1, source_target_pairs={{0,1},{1,0},{2,3},{3,2},{4,5},{5,4},{6,7},{7,6},{8,9},{9,8},{10,11... | collective-permute-start | bytes 1572872 | tf_op jit(solution)/shard_map/ppermute | solution.py:433
  72.5 18.7 %collective-permute-start.18 = (bf16[512,512]{1,0:T(8,128)(2,1)S(1)}, bf16[512,512]{1,0:T(8,128)(2,1)S(1)}, u32[]{:S(2)}, u32[]{:S(2)}) collective-permute-start(bf16[512,512]{1,0:T(8,128)(2,1)S(1)} %get-tuple-element.54.refs_2_), channel_id=1, source_target_pairs={{0,12},{1,49},{4,0},{5,53},{8,4},{9,57},{12,8},{13,61},{16,28},{17... | collective-permute-start | bytes 1572872 | tf_op jit(solution)/shard_map/ppermute | solution.py:444
  87.1 9.5 %collective-permute-start.21 = (bf16[512,512]{1,0:T(8,128)(2,1)S(1)}, bf16[512,512]{1,0:T(8,128)(2,1)S(1)}, u32[]{:S(2)}, u32[]{:S(2)}) collective-permute-start(bf16[512,512]{1,0:T(8,128)(2,1)S(1)} %get-tuple-element.54.refs_2_), channel_id=1, source_target_pairs={{0,4},{1,17},{4,8},{5,21},{8,12},{9,25},{12,0},{13,29},{16,20},{17... | collective-permute-start | bytes 1572872 | tf_op jit(solution)/shard_map/ppermute | solution.py:444
  87.1 11.2 %collective-permute-start.23 = (bf16[512,512]{1,0:T(8,128)(2,1)S(1)}, bf16[512,512]{1,0:T(8,128)(2,1)S(1)}, u32[]{:S(2)}, u32[]{:S(2)}) collective-permute-start(bf16[512,512]{1,0:T(8,128)(2,1)S(1)} %get-tuple-element.53.refs_0_), channel_id=1, source_target_pairs={{0,12},{1,49},{4,0},{5,53},{8,4},{9,57},{12,8},{13,61},{16,28},{17... | collective-permute-start | bytes 1572872 | tf_op jit(solution)/shard_map/ppermute | solution.py:444
  89.8 8.6 %collective-permute-start.25 = (bf16[512,512]{1,0:T(8,128)(2,1)S(1)}, bf16[512,512]{1,0:T(8,128)(2,1)S(1)}, u32[]{:S(2)}, u32[]{:S(2)}) collective-permute-start(bf16[512,512]{1,0:T(8,128)(2,1)S(1)} %collective-permute-done.15.refs_0_), channel_id=1, source_target_pairs={{0,1},{1,0},{2,3},{3,2},{4,5},{5,4},{6,7},{7,6},{8,9},{9,8},{10,11... | collective-permute-start | bytes 1572872 | tf_op jit(solution)/shard_map/ppermute | solution.py:433
  91.2 11.0 %collective-permute-start.16 = (bf16[512,512]{1,0:T(8,128)(2,1)S(1)}, bf16[512,512]{1,0:T(8,128)(2,1)S(1)}, u32[]{:S(2)}, u32[]{:S(2)}) collective-permute-start(bf16[512,512]{1,0:T(8,128)(2,1)S(1)} %collective-permute-done.15.refs_0_), channel_id=1, source_target_pairs={{0,4},{1,17},{4,8},{5,21},{8,12},{9,25},{12,0},{13,29},{16,20},{17... | collective-permute-start | bytes 1572872 | tf_op jit(solution)/shard_map/ppermute | solution.py:444
  91.2 12.8 %collective-permute-start.19 = (bf16[512,512]{1,0:T(8,128)(2,1)S(1)}, bf16[512,512]{1,0:T(8,128)(2,1)S(1)}, u32[]{:S(2)}, u32[]{:S(2)}) collective-permute-start(bf16[512,512]{1,0:T(8,128)(2,1)S(1)} %collective-permute-done.18.refs_2_), channel_id=1, source_target_pairs={{0,12},{1,49},{4,0},{5,53},{8,4},{9,57},{12,8},{13,61},{16,28},{17... | collective-permute-start | bytes 1572872 | tf_op jit(solution)/shard_map/ppermute | solution.py:444
  96.6 10.2 %collective-permute-start.26 = (bf16[512,512]{1,0:T(8,128)(2,1)S(1)}, bf16[512,512]{1,0:T(8,128)(2,1)S(1)}, u32[]{:S(2)}, u32[]{:S(2)}) collective-permute-start(bf16[512,512]{1,0:T(8,128)(2,1)S(1)} %collective-permute-done.18.refs_2_), channel_id=1, source_target_pairs={{0,1},{1,0},{2,3},{3,2},{4,5},{5,4},{6,7},{7,6},{8,9},{9,8},{10,11... | collective-permute-start | bytes 1572872 | tf_op jit(solution)/shard_map/ppermute | solution.py:433
  98.3 9.8 %collective-permute-start.22 = (bf16[512,512]{1,0:T(8,128)(2,1)S(1)}, bf16[512,512]{1,0:T(8,128)(2,1)S(1)}, u32[]{:S(2)}, u32[]{:S(2)}) collective-permute-start(bf16[512,512]{1,0:T(8,128)(2,1)S(1)} %collective-permute-done.21.refs_0_), channel_id=1, source_target_pairs={{0,1},{1,0},{2,3},{3,2},{4,5},{5,4},{6,7},{7,6},{8,9},{9,8},{10,11... | collective-permute-start | bytes 1572872 | tf_op jit(solution)/shard_map/ppermute | solution.py:433
  98.4 9.8 %collective-permute-start.24 = (bf16[512,512]{1,0:T(8,128)(2,1)S(1)}, bf16[512,512]{1,0:T(8,128)(2,1)S(1)}, u32[]{:S(2)}, u32[]{:S(2)}) collective-permute-start(bf16[512,512]{1,0:T(8,128)(2,1)S(1)} %collective-permute-done.23.refs_2_), channel_id=1, source_target_pairs={{0,1},{1,0},{2,3},{3,2},{4,5},{5,4},{6,7},{7,6},{8,9},{9,8},{10,11... | collective-permute-start | bytes 1572872 | tf_op jit(solution)/shard_map/ppermute | solution.py:433
  102.2 7.3 %collective-permute-start.17 = (bf16[512,512]{1,0:T(8,128)(2,1)S(1)}, bf16[512,512]{1,0:T(8,128)(2,1)S(1)}, u32[]{:S(2)}, u32[]{:S(2)}) collective-permute-start(bf16[512,512]{1,0:T(8,128)(2,1)S(1)} %collective-permute-done.16.refs_0_), channel_id=1, source_target_pairs={{0,1},{1,0},{2,3},{3,2},{4,5},{5,4},{6,7},{7,6},{8,9},{9,8},{10,11... | collective-permute-start | bytes 1572872 | tf_op jit(solution)/shard_map/ppermute | solution.py:433
  104.0 5.6 %collective-permute-start.20 = (bf16[512,512]{1,0:T(8,128)(2,1)S(1)}, bf16[512,512]{1,0:T(8,128)(2,1)S(1)}, u32[]{:S(2)}, u32[]{:S(2)}) collective-permute-start(bf16[512,512]{1,0:T(8,128)(2,1)S(1)} %collective-permute-done.19.refs_2_), channel_id=1, source_target_pairs={{0,1},{1,0},{2,3},{3,2},{4,5},{5,4},{6,7},{7,6},{8,9},{9,8},{10,11... | collective-permute-start | bytes 1572872 | tf_op jit(solution)/shard_map/ppermute | solution.py:433
  (4 other events, 23.9 us)
where the time goes:
time: 111 us
  waiting for transfers between devices  45.5 us (41%)
  starting transfers between devices  41.4 us (37%)
  Pallas kernels  22.5 us (20%)
    ppermute x18, waiting for transfers between devices, ring(): return lax.ppermute(value, ('z', 'x', 'c'), pairs)  28.8 us
    ppermute x18, starting transfers between devices, ring(): return lax.ppermute(value, ('z', 'x', 'c'), pairs)  26 us
    ppermute x11, starting transfers between devices, swap(): return lax.ppermute(value, axis, [(0, 1), (1, 0)])  12.8 us
    ppermute x2, waiting for transfers between devices, down(): return lax.ppermute(value, 's', [(1, 0)])  12.1 us
    pallas_call x4, Pallas kernels, assemble(): pl.pallas_call(body, in_specs=[vmem()] * (2 * count) + [anywhere] * extra...  5.51 us
    pallas_call x1, Pallas kernels, project(): pl.pallas_call(project_body, in_specs=[anywhere, vmem(), anywhere, anywhe...  5.08 us
    ppermute x11, waiting for transfers between devices, swap(): return lax.ppermute(value, axis, [(0, 1), (1, 0)])  4.61 us
    pallas_call x1, Pallas kernels, attend(): pl.pallas_call(attend_body, in_specs=[vmem()] * 4, out_specs=[vmem()] * 5...  4.02 us
  transfers between devices with their start and end apart: 31, of which 13 were waited for; matrix products, arithmetic and copies ran while one was open for 0% of the time, Pallas kernels for 14%

commit v1 on v0

--- a/solution.py
+++ b/solution.py
@@ -52,7 +52,7 @@
     return pltpu.CompilerParams(vmem_limit_bytes=mebibytes << 20)
 
 
-def project_body(x, gain, wk, wv, normed, keys, values, inverse, xs, wks, wvs, sems):
+def project_body(x, gain_row, wk, wv, normed, keys, values, inverse, xs, wks, wvs, gain, sems):
     copies = [
         pltpu.make_async_copy(x.at[pl.ds(64 * i, 64), :], xs.at[pl.ds(64 * i, 64), :], sems.at[i])
         for i in range(4)
@@ -61,8 +61,11 @@
         part = pl.ds(512 * i, 512)
         copies.append(pltpu.make_async_copy(wk.at[part, :], wks.at[part, :], sems.at[4 + 2 * i]))
         copies.append(pltpu.make_async_copy(wv.at[part, :], wvs.at[part, :], sems.at[5 + 2 * i]))
+    gain_copy = pltpu.make_async_copy(gain_row, gain, sems.at[20])
+    gain_copy.start()
     for copy in copies:
         copy.start()
+    gain_copy.wait()
     for i in range(4):
         copies[i].wait()
         rows = slice(64 * i, 64 * i + 64)
@@ -89,7 +92,7 @@
     anywhere = pl.BlockSpec(memory_space=pl.ANY)
     return pl.pallas_call(
         project_body,
-        in_specs=[anywhere, vmem(), anywhere, anywhere],
+        in_specs=[anywhere] * 4,
         out_specs=[vmem()] * 7,
         out_shape=[
             held((ROWS, WIDTH), bf16),
@@ -100,11 +103,11 @@
             held((WIDTH, COLS), bf16),
             held((WIDTH, COLS), bf16),
         ],
-        scratch_shapes=[pltpu.SemaphoreType.DMA((20,))],
+        scratch_shapes=[pltpu.VMEM((1, WIDTH), f32), pltpu.SemaphoreType.DMA((21,))],
         cost_estimate=pl.CostEstimate(flops=2 * ROWS * WIDTH * 1024, bytes_accessed=12 << 20, transcendentals=0),
         name="project",
         compiler_params=budget(16),
-    )(*far(x), *hold(gain), *far(wk, wv))
+    )(*far(x, gain, wk, wv))
 
 
 def attend_body(q, og, kf, vf, gk, gv, keep, send, row):

time: 111 us -> 111 us (level)
  no operation moved by 1% of the time
where the time goes in v1:
time: 111 us; the launch traced here: 110 us
  waiting for transfers between devices  45.6 us (41%)
  starting transfers between devices  41.3 us (37%)
  Pallas kernels  22.5 us (20%)
    ppermute x18, waiting for transfers between devices, ring(): return lax.ppermute(value, ('z', 'x', 'c'), pairs)  28.9 us
    ppermute x18, starting transfers between devices, ring(): return lax.ppermute(value, ('z', 'x', 'c'), pairs)  26 us
    ppermute x11, starting transfers between devices, swap(): return lax.ppermute(value, axis, [(0, 1), (1, 0)])  12.7 us
    ppermute x2, waiting for transfers between devices, down(): return lax.ppermute(value, 's', [(1, 0)])  12.1 us
    pallas_call x4, Pallas kernels, assemble(): pl.pallas_call(body, in_specs=[vmem()] * (2 * count) + [anywhere] * extra...  5.51 us
    pallas_call x1, Pallas kernels, project(): pl.pallas_call(project_body, in_specs=[anywhere] * 4, out_specs=[vmem()]...  5.1 us
    ppermute x11, waiting for transfers between devices, swap(): return lax.ppermute(value, axis, [(0, 1), (1, 0)])  4.63 us
    pallas_call x1, Pallas kernels, attend(): pl.pallas_call(attend_body, in_specs=[vmem()] * 4, out_specs=[vmem()] * 5...  4.02 us
  transfers between devices with their start and end apart: 31, of which 13 were waited for; matrix products, arithmetic and copies ran while one was open for 0% of the time, Pallas kernels for 14%

profile of v1, /device:TPU:1, one launch (start us, length us, event | category | flops | bytes accessed | tf_op | source)
XLA Modules:
  0.0 110.5 jit_solution(10394128289442860742)
XLA Ops:
  0.7 5.1 %project.1 = (bf16[256,4096]{1,0:T(8,128)(2,1)S(1)}, f32[256,512]{1,0:T(8,128)S(1)}, f32[256,512]{1,0:T(8,128)S(1)}, f32[256,128]{1,0:T(8,128)S(1)}, bf16[256,40...) custom-call(bf16[256,4096]{1,0:T(8,128)(2,1)} %bitcast.14, f32[1,4096]{1,0:T(1,128)} %gain.1, ...), custom_call_target="tpu_custom_call" | custom-call | flops 2147483648 | bytes 12582912 | tf_op jit(solution)/shard_map/project/pallas_call | solution.py:93
  5.8 1.5 %collective-permute-start = (bf16[256,4096]{1,0:T(8,128)(2,1)S(1)}, bf16[256,4096]{1,0:T(8,128)(2,1)S(1)}, u32[]{:S(2)}, u32[]{:S(2)}) collective-permute-start(bf16[256,4096]{1,0:T(8,128)(2,1)S(1)} %get-tuple-element.38.mine), channel_id=1, source_target_pairs={{0,1},{1,0},{2,3},{3,2},{4,5},{5,4},{6,7},{7,6},{8,9},{9,8},{10,11... | collective-permute-start | bytes 6291464 | tf_op jit(solution)/shard_map/ppermute | solution.py:436
  7.2 4.0 %attend.1 = (bf16[256,512]{1,0:T(8,128)(2,1)S(1)}, bf16[256,512]{1,0:T(8,128)(2,1)S(1)}, bf16[256,512]{1,0:T(8,128)(2,1)S(1)}, bf16[256,512]{1,0:T(8,128)(2,1)S(1)}, f32[256,128]{1,0:T(8,128)S(1)}) custom-call(bf16[256,2048]{1,0:T(8,128)(2,1)S(1)} %bitcast.8, bf16[256,2048]{1,0:T(8,128)(2,1)S(1)} %bitcast.9, f32[256,512]{1,0:T(8,128)S(1)} %get-tuple-element.39.kf, ...), custom_call_target="tpu_custom_call" | custom-call | flops 2400000000 | bytes 4194304 | tf_op jit(solution)/shard_map/attend/pallas_call | solution.py:154
  11.4 1.5 %collective-permute-done.1.grad_theirs = bf16[256,512]{1,0:T(8,128)(2,1)S(1)} collective-permute-done((bf16[256,512]{1,0:T(8,128)(2,1)S(1)}, bf16[256,512]{1,0:T(8,128)(2,1)S(1)}, u32[]{:S(2)}, u32[]{:S(2)}) %collective-permute-start.1) | collective-permute-done | bytes 262176 | tf_op jit(solution)/shard_map/ppermute | solution.py:436
  13.6 3.9 %collective-permute-start.6 = (bf16[512,512]{1,0:T(8,128)(2,1)S(1)}, bf16[512,512]{1,0:T(8,128)(2,1)S(1)}, u32[]{:S(2)}, u32[]{:S(2)}) collective-permute-start(bf16[512,512]{1,0:T(8,128)(2,1)S(1)} %get-tuple-element.48), channel_id=1, source_target_pairs={{0,12},{1,49},{4,0},{5,53},{8,4},{9,57},{12,8},{13,61},{16,28},{17... | collective-permute-start | bytes 1572872 | tf_op jit(solution)/shard_map/ppermute | solution.py:447
  19.0 2.7 %collective-permute-start.5 = (bf16[512,512]{1,0:T(8,128)(2,1)S(1)}, bf16[512,512]{1,0:T(8,128)(2,1)S(1)}, u32[]{:S(2)}, u32[]{:S(2)}) collective-permute-start(bf16[512,512]{1,0:T(8,128)(2,1)S(1)} %get-tuple-element.46), channel_id=1, source_target_pairs={{0,12},{1,49},{4,0},{5,53},{8,4},{9,57},{12,8},{13,61},{16,28},{17... | collective-permute-start | bytes 1572872 | tf_op jit(solution)/shard_map/ppermute | solution.py:447
  21.7 2.0 %collective-permute-done.6.arrived = bf16[512,512]{1,0:T(8,128)(2,1)S(1)} collective-permute-done((bf16[512,512]{1,0:T(8,128)(2,1)S(1)}, bf16[512,512]{1,0:T(8,128)(2,1)S(1)}, u32[]{:S(2)}, u32[]{:S(2)}) %collective-permute-start.6) | collective-permute-done | bytes 524320 | tf_op jit(solution)/shard_map/ppermute | solution.py:447
  23.8 3.5 %collective-permute-start.7 = (bf16[512,512]{1,0:T(8,128)(2,1)S(1)}, bf16[512,512]{1,0:T(8,128)(2,1)S(1)}, u32[]{:S(2)}, u32[]{:S(2)}) collective-permute-start(bf16[512,512]{1,0:T(8,128)(2,1)S(1)} %relay.3), channel_id=1, source_target_pairs={{0,12},{1,49},{4,0},{5,53},{8,4},{9,57},{12,8},{13,61},{16,28},{17... | collective-permute-start | bytes 1572872 | tf_op jit(solution)/shard_map/ppermute | solution.py:447
  27.7 2.6 %input_terms.1 = (f32[256,4096]{1,0:T(8,128)S(1)}, bf16[128,4096]{1,0:T(8,128)(2,1)S(1)}, bf16[128,4096]{1,0:T(8,128)(2,1)S(1)}) custom-call(bf16[256,512]{1,0:T(8,128)(2,1)S(1)} %get-tuple-element.63.gk, bf16[256,512]{1,0:T(8,128)(2,1)S(1)} %get-tuple-element.64.gv, bf16[4096,512]{1,0:T(8,128)(2,1)S(1)} %get-tuple-element.65.wk, ...), custom_call_target="tpu_custom_call" | custom-call | flops 2147483648 | bytes 18874368 | tf_op jit(solution)/shard_map/input_terms/pallas_call | solution.py:278
  32.7 2.2 %collective-permute-done.7.a_bottom = bf16[512,512]{1,0:T(8,128)(2,1)S(1)} collective-permute-done((bf16[512,512]{1,0:T(8,128)(2,1)S(1)}, bf16[512,512]{1,0:T(8,128)(2,1)S(1)}, u32[]{:S(2)}, u32[]{:S(2)}) %collective-permute-start.7) | collective-permute-done | bytes 524320 | tf_op jit(solution)/shard_map/ppermute | solution.py:447
  34.9 3.4 %collective-permute-done.3.b_top = bf16[512,512]{1,0:T(8,128)(2,1)S(1)} collective-permute-done((bf16[512,512]{1,0:T(8,128)(2,1)S(1)}, bf16[512,512]{1,0:T(8,128)(2,1)S(1)}, u32[]{:S(2)}, u32[]{:S(2)}) %collective-permute-start.3) | collective-permute-done | bytes 524320 | tf_op jit(solution)/shard_map/ppermute | solution.py:447
  38.9 2.5 %collective-permute-start.10 = (bf16[256,512]{1,0:T(8,128)(2,1)S(1)}, bf16[256,512]{1,0:T(8,128)(2,1)S(1)}, u32[]{:S(2)}, u32[]{:S(2)}) collective-permute-start(bf16[256,512]{1,0:T(8,128)(2,1)S(1)} %get-tuple-element.52), channel_id=1, source_target_pairs={{0,48},{1,13},{4,52},{5,1},{8,56},{9,5},{12,60},{13,9},{16,0},{17,... | collective-permute-start | bytes 786440 | tf_op jit(solution)/shard_map/ppermute | solution.py:447
  41.5 1.7 %collective-permute-start.9 = (bf16[256,512]{1,0:T(8,128)(2,1)S(1)}, bf16[256,512]{1,0:T(8,128)(2,1)S(1)}, u32[]{:S(2)}, u32[]{:S(2)}) collective-permute-start(bf16[256,512]{1,0:T(8,128)(2,1)S(1)} %get-tuple-element.51), channel_id=1, source_target_pairs={{0,32},{1,9},{4,36},{5,13},{8,40},{9,1},{12,44},{13,5},{16,48},{17... | collective-permute-start | bytes 786440 | tf_op jit(solution)/shard_map/ppermute | solution.py:447
  43.2 1.6 %collective-permute-done.10.r3 = bf16[256,512]{1,0:T(8,128)(2,1)S(1)} collective-permute-done((bf16[256,512]{1,0:T(8,128)(2,1)S(1)}, bf16[256,512]{1,0:T(8,128)(2,1)S(1)}, u32[]{:S(2)}, u32[]{:S(2)}) %collective-permute-start.10) | collective-permute-done | bytes 262176 | tf_op jit(solution)/shard_map/ppermute | solution.py:447
  44.8 6.2 %collective-permute-done.8.r1 = bf16[256,512]{1,0:T(8,128)(2,1)S(1)} collective-permute-done((bf16[256,512]{1,0:T(8,128)(2,1)S(1)}, bf16[256,512]{1,0:T(8,128)(2,1)S(1)}, u32[]{:S(2)}, u32[]{:S(2)}) %collective-permute-start.8) | collective-permute-done | bytes 262176 | tf_op jit(solution)/shard_map/ppermute | solution.py:447
  53.6 3.1 %collective-permute-done.11.other = bf16[256,512]{1,0:T(8,128)(2,1)S(1)} collective-permute-done((bf16[256,512]{1,0:T(8,128)(2,1)S(1)}, bf16[256,512]{1,0:T(8,128)(2,1)S(1)}, u32[]{:S(2)}, u32[]{:S(2)}) %collective-permute-start.11) | collective-permute-done | bytes 262176 | tf_op jit(solution)/shard_map/ppermute | solution.py:436
  56.9 1.7 %collective-permute-start.13 = (bf16[256,512]{1,0:T(8,128)(2,1)S(1)}, bf16[256,512]{1,0:T(8,128)(2,1)S(1)}, u32[]{:S(2)}, u32[]{:S(2)}) collective-permute-start(bf16[256,512]{1,0:T(8,128)(2,1)S(1)} %mean.1.own), channel_id=1, source_target_pairs={{0,32},{1,9},{4,36},{5,13},{8,40},{9,1},{12,44},{13,5},{16,48},{17... | collective-permute-start | bytes 786440 | tf_op jit(solution)/shard_map/ppermute | solution.py:447
  58.6 1.6 %collective-permute-start.14 = (bf16[256,512]{1,0:T(8,128)(2,1)S(1)}, bf16[256,512]{1,0:T(8,128)(2,1)S(1)}, u32[]{:S(2)}, u32[]{:S(2)}) collective-permute-start(bf16[256,512]{1,0:T(8,128)(2,1)S(1)} %mean.1.own), channel_id=1, source_target_pairs={{0,48},{1,13},{4,52},{5,1},{8,56},{9,5},{12,60},{13,9},{16,0},{17,... | collective-permute-start | bytes 786440 | tf_op jit(solution)/shard_map/ppermute | solution.py:447
  60.2 6.2 %collective-permute-done.12.r1 = bf16[256,512]{1,0:T(8,128)(2,1)S(1)} collective-permute-done((bf16[256,512]{1,0:T(8,128)(2,1)S(1)}, bf16[256,512]{1,0:T(8,128)(2,1)S(1)}, u32[]{:S(2)}, u32[]{:S(2)}) %collective-permute-start.12) | collective-permute-done | bytes 262176 | tf_op jit(solution)/shard_map/ppermute | solution.py:447
  67.2 4.5 %collective-permute-start.27 = (bf16[512,512]{1,0:T(8,128)(2,1)S(1)}, bf16[512,512]{1,0:T(8,128)(2,1)S(1)}, u32[]{:S(2)}, u32[]{:S(2)}) collective-permute-start(bf16[512,512]{1,0:T(8,128)(2,1)S(1)} %get-tuple-element.53.refs_0_), channel_id=1, source_target_pairs={{0,1},{1,0},{2,3},{3,2},{4,5},{5,4},{6,7},{7,6},{8,9},{9,8},{10,11... | collective-permute-start | bytes 1572872 | tf_op jit(solution)/shard_map/ppermute | solution.py:436
  71.9 2.5 %collective-permute-start.18 = (bf16[512,512]{1,0:T(8,128)(2,1)S(1)}, bf16[512,512]{1,0:T(8,128)(2,1)S(1)}, u32[]{:S(2)}, u32[]{:S(2)}) collective-permute-start(bf16[512,512]{1,0:T(8,128)(2,1)S(1)} %get-tuple-element.54.refs_2_), channel_id=1, source_target_pairs={{0,12},{1,49},{4,0},{5,53},{8,4},{9,57},{12,8},{13,61},{16,28},{17... | collective-permute-start | bytes 1572872 | tf_op jit(solution)/shard_map/ppermute | solution.py:447
  74.4 12.1 %collective-permute-done.30.upper = bf16[128,4096]{1,0:T(8,128)(2,1)S(1)} collective-permute-done((bf16[128,4096]{1,0:T(8,128)(2,1)S(1)}, bf16[128,4096]{1,0:T(8,128)(2,1)S(1)}, u32[]{:S(2)}, u32[]{:S(2)}) %collective-permute-start.30) | collective-permute-done | bytes 1048608 | tf_op jit(solution)/shard_map/ppermute | solution.py:451
  86.4 2.7 %collective-permute-start.23 = (bf16[512,512]{1,0:T(8,128)(2,1)S(1)}, bf16[512,512]{1,0:T(8,128)(2,1)S(1)}, u32[]{:S(2)}, u32[]{:S(2)}) collective-permute-start(bf16[512,512]{1,0:T(8,128)(2,1)S(1)} %get-tuple-element.53.refs_0_), channel_id=1, source_target_pairs={{0,12},{1,49},{4,0},{5,53},{8,4},{9,57},{12,8},{13,61},{16,28},{17... | collective-permute-start | bytes 1572872 | tf_op jit(solution)/shard_map/ppermute | solution.py:447
  89.1 1.4 %collective-permute-start.25 = (bf16[512,512]{1,0:T(8,128)(2,1)S(1)}, bf16[512,512]{1,0:T(8,128)(2,1)S(1)}, u32[]{:S(2)}, u32[]{:S(2)}) collective-permute-start(bf16[512,512]{1,0:T(8,128)(2,1)S(1)} %collective-permute-done.15.refs_0_), channel_id=1, source_target_pairs={{0,1},{1,0},{2,3},{3,2},{4,5},{5,4},{6,7},{7,6},{8,9},{9,8},{10,11... | collective-permute-start | bytes 1572872 | tf_op jit(solution)/shard_map/ppermute | solution.py:436
  90.5 2.7 %collective-permute-start.19 = (bf16[512,512]{1,0:T(8,128)(2,1)S(1)}, bf16[512,512]{1,0:T(8,128)(2,1)S(1)}, u32[]{:S(2)}, u32[]{:S(2)}) collective-permute-start(bf16[512,512]{1,0:T(8,128)(2,1)S(1)} %collective-permute-done.18.refs_2_), channel_id=1, source_target_pairs={{0,12},{1,49},{4,0},{5,53},{8,4},{9,57},{12,8},{13,61},{16,28},{17... | collective-permute-start | bytes 1572872 | tf_op jit(solution)/shard_map/ppermute | solution.py:447
  93.3 2.7 %collective-permute-done.21.refs_0_ = bf16[512,512]{1,0:T(8,128)(2,1)S(1)} collective-permute-done((bf16[512,512]{1,0:T(8,128)(2,1)S(1)}, bf16[512,512]{1,0:T(8,128)(2,1)S(1)}, u32[]{:S(2)}, u32[]{:S(2)}) %collective-permute-start.21) | collective-permute-done | bytes 524320 | tf_op jit(solution)/shard_map/ppermute | solution.py:447
  96.0 1.7 %collective-permute-start.26 = (bf16[512,512]{1,0:T(8,128)(2,1)S(1)}, bf16[512,512]{1,0:T(8,128)(2,1)S(1)}, u32[]{:S(2)}, u32[]{:S(2)}) collective-permute-start(bf16[512,512]{1,0:T(8,128)(2,1)S(1)} %collective-permute-done.18.refs_2_), channel_id=1, source_target_pairs={{0,1},{1,0},{2,3},{3,2},{4,5},{5,4},{6,7},{7,6},{8,9},{9,8},{10,11... | collective-permute-start | bytes 1572872 | tf_op jit(solution)/shard_map/ppermute | solution.py:436
  98.2 3.4 %collective-permute-done.16.refs_0_ = bf16[512,512]{1,0:T(8,128)(2,1)S(1)} collective-permute-done((bf16[512,512]{1,0:T(8,128)(2,1)S(1)}, bf16[512,512]{1,0:T(8,128)(2,1)S(1)}, u32[]{:S(2)}, u32[]{:S(2)}) %collective-permute-start.16) | collective-permute-done | bytes 524320 | tf_op jit(solution)/shard_map/ppermute | solution.py:447
  101.6 1.7 %collective-permute-start.17 = (bf16[512,512]{1,0:T(8,128)(2,1)S(1)}, bf16[512,512]{1,0:T(8,128)(2,1)S(1)}, u32[]{:S(2)}, u32[]{:S(2)}) collective-permute-start(bf16[512,512]{1,0:T(8,128)(2,1)S(1)} %collective-permute-done.16.refs_0_), channel_id=1, source_target_pairs={{0,1},{1,0},{2,3},{3,2},{4,5},{5,4},{6,7},{7,6},{8,9},{9,8},{10,11... | collective-permute-start | bytes 1572872 | tf_op jit(solution)/shard_map/ppermute | solution.py:436
  103.3 1.4 %finish.1 = bf16[256,4096]{1,0:T(8,128)(2,1)} custom-call(f32[256,4096]{1,0:T(8,128)S(1)} %get-tuple-element.70.own, bf16[128,4096]{1,0:T(8,128)(2,1)S(1)} %collective-permute-done.29.lower, bf16[128,4096]{1,0:T(8,128)(2,1)S(1)} %collective-permute-done.30.upper), custom_call_target="tpu_custom_call" | custom-call | flops 1048576 | bytes 8388608 | tf_op jit(solution)/shard_map/finish/pallas_call | solution.py:306
  106.1 1.4 %assemble.5 = (bf16[4096,512]{1,0:T(8,128)(2,1)}, bf16[4096,512]{1,0:T(8,128)(2,1)}) custom-call(bf16[512,512]{1,0:T(8,128)(2,1)S(1)} %collective-permute-done.15.refs_0_, bf16[512,512]{1,0:T(8,128)(2,1)S(1)} %collective-permute-done.25.refs_1_, bf16[512,512]{1,0:T(8,128)(2,1)S(1)} %collective-permute-done.18.refs_2_, ...), custom_call_target="tpu_custom_call", output_to_operand_aliasing={{0}: (4, {}), {1}: (5, {})} | custom-call | tf_op jit(solution)/shard_map/assemble/pallas_call | solution.py:423
  107.5 1.4 %assemble.6 = (bf16[4096,512]{1,0:T(8,128)(2,1)}, bf16[4096,512]{1,0:T(8,128)(2,1)}) custom-call(bf16[512,512]{1,0:T(8,128)(2,1)S(1)} %collective-permute-done.21.refs_0_, bf16[512,512]{1,0:T(8,128)(2,1)S(1)} %collective-permute-done.22.refs_1_, bf16[512,512]{1,0:T(8,128)(2,1)S(1)} %collective-permute-done.23.refs_2_, ...), custom_call_target="tpu_custom_call", output_to_operand_aliasing={{0}: (4, {}), {1}: (5, {})} | custom-call | tf_op jit(solution)/shard_map/assemble/pallas_call | solution.py:423
  (55 shorter events, 12.8 us)
Async XLA Ops:
  5.8 7.1 %collective-permute-start = (bf16[256,4096]{1,0:T(8,128)(2,1)S(1)}, bf16[256,4096]{1,0:T(8,128)(2,1)S(1)}, u32[]{:S(2)}, u32[]{:S(2)}) collective-permute-start(bf16[256,4096]{1,0:T(8,128)(2,1)S(1)} %get-tuple-element.38.mine), channel_id=1, source_target_pairs={{0,1},{1,0},{2,3},{3,2},{4,5},{5,4},{6,7},{7,6},{8,9},{9,8},{10,11... | collective-permute-start | bytes 6291464 | tf_op jit(solution)/shard_map/ppermute | solution.py:436
  11.3 1.6 %collective-permute-start.1 = (bf16[256,512]{1,0:T(8,128)(2,1)S(1)}, bf16[256,512]{1,0:T(8,128)(2,1)S(1)}, u32[]{:S(2)}, u32[]{:S(2)}) collective-permute-start(bf16[256,512]{1,0:T(8,128)(2,1)S(1)} %get-tuple-element.42), channel_id=1, source_target_pairs={{0,1},{1,0},{2,3},{3,2},{4,5},{5,4},{6,7},{7,6},{8,9},{9,8},{10,11... | collective-permute-start | bytes 786440 | tf_op jit(solution)/shard_map/ppermute | solution.py:436
  13.6 10.1 %collective-permute-start.6 = (bf16[512,512]{1,0:T(8,128)(2,1)S(1)}, bf16[512,512]{1,0:T(8,128)(2,1)S(1)}, u32[]{:S(2)}, u32[]{:S(2)}) collective-permute-start(bf16[512,512]{1,0:T(8,128)(2,1)S(1)} %get-tuple-element.48), channel_id=1, source_target_pairs={{0,12},{1,49},{4,0},{5,53},{8,4},{9,57},{12,8},{13,61},{16,28},{17... | collective-permute-start | bytes 1572872 | tf_op jit(solution)/shard_map/ppermute | solution.py:447
  17.6 10.1 %copy-start.1 = (f32[1,4096]{1,0:T(1,128)S(1)}, f32[1,4096]{1,0:T(1,128)}, u32[]{:S(2)}) copy-start(f32[1,4096]{1,0:T(1,128)} %gain.1) | copy-start | bytes 49156
  17.6 9.7 %collective-permute-start.2 = (bf16[512,512]{1,0:T(8,128)(2,1)S(1)}, bf16[512,512]{1,0:T(8,128)(2,1)S(1)}, u32[]{:S(2)}, u32[]{:S(2)}) collective-permute-start(bf16[512,512]{1,0:T(8,128)(2,1)S(1)} %get-tuple-element.44), channel_id=1, source_target_pairs={{0,4},{1,17},{4,8},{5,21},{8,12},{9,25},{12,0},{13,29},{16,20},{17... | collective-permute-start | bytes 1572872 | tf_op jit(solution)/shard_map/ppermute | solution.py:447
  18.9 13.8 %collective-permute-start.4 = (bf16[512,512]{1,0:T(8,128)(2,1)S(1)}, bf16[512,512]{1,0:T(8,128)(2,1)S(1)}, u32[]{:S(2)}, u32[]{:S(2)}) collective-permute-start(bf16[512,512]{1,0:T(8,128)(2,1)S(1)} %get-tuple-element.45), channel_id=1, source_target_pairs={{0,4},{1,17},{4,8},{5,21},{8,12},{9,25},{12,0},{13,29},{16,20},{17... | collective-permute-start | bytes 1572872 | tf_op jit(solution)/shard_map/ppermute | solution.py:447
  19.0 13.8 %collective-permute-start.5 = (bf16[512,512]{1,0:T(8,128)(2,1)S(1)}, bf16[512,512]{1,0:T(8,128)(2,1)S(1)}, u32[]{:S(2)}, u32[]{:S(2)}) collective-permute-start(bf16[512,512]{1,0:T(8,128)(2,1)S(1)} %get-tuple-element.46), channel_id=1, source_target_pairs={{0,12},{1,49},{4,0},{5,53},{8,4},{9,57},{12,8},{13,61},{16,28},{17... | collective-permute-start | bytes 1572872 | tf_op jit(solution)/shard_map/ppermute | solution.py:447
  23.8 11.1 %collective-permute-start.7 = (bf16[512,512]{1,0:T(8,128)(2,1)S(1)}, bf16[512,512]{1,0:T(8,128)(2,1)S(1)}, u32[]{:S(2)}, u32[]{:S(2)}) collective-permute-start(bf16[512,512]{1,0:T(8,128)(2,1)S(1)} %relay.3), channel_id=1, source_target_pairs={{0,12},{1,49},{4,0},{5,53},{8,4},{9,57},{12,8},{13,61},{16,28},{17... | collective-permute-start | bytes 1572872 | tf_op jit(solution)/shard_map/ppermute | solution.py:447
  27.4 11.0 %collective-permute-start.3 = (bf16[512,512]{1,0:T(8,128)(2,1)S(1)}, bf16[512,512]{1,0:T(8,128)(2,1)S(1)}, u32[]{:S(2)}, u32[]{:S(2)}) collective-permute-start(bf16[512,512]{1,0:T(8,128)(2,1)S(1)} %relay.2), channel_id=1, source_target_pairs={{0,4},{1,17},{4,8},{5,21},{8,12},{9,25},{12,0},{13,29},{16,20},{17... | collective-permute-start | bytes 1572872 | tf_op jit(solution)/shard_map/ppermute | solution.py:447
  30.2 41.6 %collective-permute-start.29 = (bf16[128,4096]{1,0:T(8,128)(2,1)S(1)}, bf16[128,4096]{1,0:T(8,128)(2,1)S(1)}, u32[]{:S(2)}, u32[]{:S(2)}) collective-permute-start(bf16[128,4096]{1,0:T(8,128)(2,1)S(1)} %get-tuple-element.71), channel_id=1, source_target_pairs={{64,0},{65,1},{66,2},{67,3},{68,4},{69,5},{70,6},{71,7},{72,8},{73... | collective-permute-start | bytes 3145736 | tf_op jit(solution)/shard_map/ppermute | solution.py:451
  38.9 5.9 %collective-permute-start.10 = (bf16[256,512]{1,0:T(8,128)(2,1)S(1)}, bf16[256,512]{1,0:T(8,128)(2,1)S(1)}, u32[]{:S(2)}, u32[]{:S(2)}) collective-permute-start(bf16[256,512]{1,0:T(8,128)(2,1)S(1)} %get-tuple-element.52), channel_id=1, source_target_pairs={{0,48},{1,13},{4,52},{5,1},{8,56},{9,5},{12,60},{13,9},{16,0},{17,... | collective-permute-start | bytes 786440 | tf_op jit(solution)/shard_map/ppermute | solution.py:447
  41.5 9.5 %collective-permute-start.8 = (bf16[256,512]{1,0:T(8,128)(2,1)S(1)}, bf16[256,512]{1,0:T(8,128)(2,1)S(1)}, u32[]{:S(2)}, u32[]{:S(2)}) collective-permute-start(bf16[256,512]{1,0:T(8,128)(2,1)S(1)} %get-tuple-element.50), channel_id=1, source_target_pairs={{0,16},{1,5},{4,20},{5,9},{8,24},{9,13},{12,28},{13,1},{16,32},{17... | collective-permute-start | bytes 786440 | tf_op jit(solution)/shard_map/ppermute | solution.py:447
  41.5 9.5 %collective-permute-start.9 = (bf16[256,512]{1,0:T(8,128)(2,1)S(1)}, bf16[256,512]{1,0:T(8,128)(2,1)S(1)}, u32[]{:S(2)}, u32[]{:S(2)}) collective-permute-start(bf16[256,512]{1,0:T(8,128)(2,1)S(1)} %get-tuple-element.51), channel_id=1, source_target_pairs={{0,32},{1,9},{4,36},{5,13},{8,40},{9,1},{12,44},{13,5},{16,48},{17... | collective-permute-start | bytes 786440 | tf_op jit(solution)/shard_map/ppermute | solution.py:447
  51.1 5.6 %collective-permute-start.11 = (bf16[256,512]{1,0:T(8,128)(2,1)S(1)}, bf16[256,512]{1,0:T(8,128)(2,1)S(1)}, u32[]{:S(2)}, u32[]{:S(2)}) collective-permute-start(bf16[256,512]{1,0:T(8,128)(2,1)S(1)} %total.1.own), channel_id=1, source_target_pairs={{0,2},{2,0},{1,3},{3,1},{4,6},{6,4},{5,7},{7,5},{8,10},{10,8},{9,1... | collective-permute-start | bytes 786440 | tf_op jit(solution)/shard_map/ppermute | solution.py:436
  52.3 34.1 %collective-permute-start.30 = (bf16[128,4096]{1,0:T(8,128)(2,1)S(1)}, bf16[128,4096]{1,0:T(8,128)(2,1)S(1)}, u32[]{:S(2)}, u32[]{:S(2)}) collective-permute-start(bf16[128,4096]{1,0:T(8,128)(2,1)S(1)} %get-tuple-element.72), channel_id=1, source_target_pairs={{64,0},{65,1},{66,2},{67,3},{68,4},{69,5},{70,6},{71,7},{72,8},{73... | collective-permute-start | bytes 3145736 | tf_op jit(solution)/shard_map/ppermute | solution.py:451
  56.8 9.6 %collective-permute-start.12 = (bf16[256,512]{1,0:T(8,128)(2,1)S(1)}, bf16[256,512]{1,0:T(8,128)(2,1)S(1)}, u32[]{:S(2)}, u32[]{:S(2)}) collective-permute-start(bf16[256,512]{1,0:T(8,128)(2,1)S(1)} %mean.1.own), channel_id=1, source_target_pairs={{0,16},{1,5},{4,20},{5,9},{8,24},{9,13},{12,28},{13,1},{16,32},{17... | collective-permute-start | bytes 786440 | tf_op jit(solution)/shard_map/ppermute | solution.py:447
  56.9 9.5 %collective-permute-start.13 = (bf16[256,512]{1,0:T(8,128)(2,1)S(1)}, bf16[256,512]{1,0:T(8,128)(2,1)S(1)}, u32[]{:S(2)}, u32[]{:S(2)}) collective-permute-start(bf16[256,512]{1,0:T(8,128)(2,1)S(1)} %mean.1.own), channel_id=1, source_target_pairs={{0,32},{1,9},{4,36},{5,13},{8,40},{9,1},{12,44},{13,5},{16,48},{17... | collective-permute-start | bytes 786440 | tf_op jit(solution)/shard_map/ppermute | solution.py:447
  58.6 8.4 %collective-permute-start.14 = (bf16[256,512]{1,0:T(8,128)(2,1)S(1)}, bf16[256,512]{1,0:T(8,128)(2,1)S(1)}, u32[]{:S(2)}, u32[]{:S(2)}) collective-permute-start(bf16[256,512]{1,0:T(8,128)(2,1)S(1)} %mean.1.own), channel_id=1, source_target_pairs={{0,48},{1,13},{4,52},{5,1},{8,56},{9,5},{12,60},{13,9},{16,0},{17,... | collective-permute-start | bytes 786440 | tf_op jit(solution)/shard_map/ppermute | solution.py:447
  67.2 19.2 %collective-permute-start.27 = (bf16[512,512]{1,0:T(8,128)(2,1)S(1)}, bf16[512,512]{1,0:T(8,128)(2,1)S(1)}, u32[]{:S(2)}, u32[]{:S(2)}) collective-permute-start(bf16[512,512]{1,0:T(8,128)(2,1)S(1)} %get-tuple-element.53.refs_0_), channel_id=1, source_target_pairs={{0,1},{1,0},{2,3},{3,2},{4,5},{5,4},{6,7},{7,6},{8,9},{9,8},{10,11... | collective-permute-start | bytes 1572872 | tf_op jit(solution)/shard_map/ppermute | solution.py:436
  71.7 17.4 %collective-permute-start.15 = (bf16[512,512]{1,0:T(8,128)(2,1)S(1)}, bf16[512,512]{1,0:T(8,128)(2,1)S(1)}, u32[]{:S(2)}, u32[]{:S(2)}) collective-permute-start(bf16[512,512]{1,0:T(8,128)(2,1)S(1)} %get-tuple-element.53.refs_0_), channel_id=1, source_target_pairs={{0,4},{1,17},{4,8},{5,21},{8,12},{9,25},{12,0},{13,29},{16,20},{17... | collective-permute-start | bytes 1572872 | tf_op jit(solution)/shard_map/ppermute | solution.py:447
  71.7 18.9 %collective-permute-start.28 = (bf16[512,512]{1,0:T(8,128)(2,1)S(1)}, bf16[512,512]{1,0:T(8,128)(2,1)S(1)}, u32[]{:S(2)}, u32[]{:S(2)}) collective-permute-start(bf16[512,512]{1,0:T(8,128)(2,1)S(1)} %get-tuple-element.54.refs_2_), channel_id=1, source_target_pairs={{0,1},{1,0},{2,3},{3,2},{4,5},{5,4},{6,7},{7,6},{8,9},{9,8},{10,11... | collective-permute-start | bytes 1572872 | tf_op jit(solution)/shard_map/ppermute | solution.py:436
  71.9 18.7 %collective-permute-start.18 = (bf16[512,512]{1,0:T(8,128)(2,1)S(1)}, bf16[512,512]{1,0:T(8,128)(2,1)S(1)}, u32[]{:S(2)}, u32[]{:S(2)}) collective-permute-start(bf16[512,512]{1,0:T(8,128)(2,1)S(1)} %get-tuple-element.54.refs_2_), channel_id=1, source_target_pairs={{0,12},{1,49},{4,0},{5,53},{8,4},{9,57},{12,8},{13,61},{16,28},{17... | collective-permute-start | bytes 1572872 | tf_op jit(solution)/shard_map/ppermute | solution.py:447
  86.4 9.5 %collective-permute-start.21 = (bf16[512,512]{1,0:T(8,128)(2,1)S(1)}, bf16[512,512]{1,0:T(8,128)(2,1)S(1)}, u32[]{:S(2)}, u32[]{:S(2)}) collective-permute-start(bf16[512,512]{1,0:T(8,128)(2,1)S(1)} %get-tuple-element.54.refs_2_), channel_id=1, source_target_pairs={{0,4},{1,17},{4,8},{5,21},{8,12},{9,25},{12,0},{13,29},{16,20},{17... | collective-permute-start | bytes 1572872 | tf_op jit(solution)/shard_map/ppermute | solution.py:447
  86.4 11.2 %collective-permute-start.23 = (bf16[512,512]{1,0:T(8,128)(2,1)S(1)}, bf16[512,512]{1,0:T(8,128)(2,1)S(1)}, u32[]{:S(2)}, u32[]{:S(2)}) collective-permute-start(bf16[512,512]{1,0:T(8,128)(2,1)S(1)} %get-tuple-element.53.refs_0_), channel_id=1, source_target_pairs={{0,12},{1,49},{4,0},{5,53},{8,4},{9,57},{12,8},{13,61},{16,28},{17... | collective-permute-start | bytes 1572872 | tf_op jit(solution)/shard_map/ppermute | solution.py:447
  89.1 8.6 %collective-permute-start.25 = (bf16[512,512]{1,0:T(8,128)(2,1)S(1)}, bf16[512,512]{1,0:T(8,128)(2,1)S(1)}, u32[]{:S(2)}, u32[]{:S(2)}) collective-permute-start(bf16[512,512]{1,0:T(8,128)(2,1)S(1)} %collective-permute-done.15.refs_0_), channel_id=1, source_target_pairs={{0,1},{1,0},{2,3},{3,2},{4,5},{5,4},{6,7},{7,6},{8,9},{9,8},{10,11... | collective-permute-start | bytes 1572872 | tf_op jit(solution)/shard_map/ppermute | solution.py:436
  90.5 11.1 %collective-permute-start.16 = (bf16[512,512]{1,0:T(8,128)(2,1)S(1)}, bf16[512,512]{1,0:T(8,128)(2,1)S(1)}, u32[]{:S(2)}, u32[]{:S(2)}) collective-permute-start(bf16[512,512]{1,0:T(8,128)(2,1)S(1)} %collective-permute-done.15.refs_0_), channel_id=1, source_target_pairs={{0,4},{1,17},{4,8},{5,21},{8,12},{9,25},{12,0},{13,29},{16,20},{17... | collective-permute-start | bytes 1572872 | tf_op jit(solution)/shard_map/ppermute | solution.py:447
  90.5 12.8 %collective-permute-start.19 = (bf16[512,512]{1,0:T(8,128)(2,1)S(1)}, bf16[512,512]{1,0:T(8,128)(2,1)S(1)}, u32[]{:S(2)}, u32[]{:S(2)}) collective-permute-start(bf16[512,512]{1,0:T(8,128)(2,1)S(1)} %collective-permute-done.18.refs_2_), channel_id=1, source_target_pairs={{0,12},{1,49},{4,0},{5,53},{8,4},{9,57},{12,8},{13,61},{16,28},{17... | collective-permute-start | bytes 1572872 | tf_op jit(solution)/shard_map/ppermute | solution.py:447
  96.0 10.1 %collective-permute-start.26 = (bf16[512,512]{1,0:T(8,128)(2,1)S(1)}, bf16[512,512]{1,0:T(8,128)(2,1)S(1)}, u32[]{:S(2)}, u32[]{:S(2)}) collective-permute-start(bf16[512,512]{1,0:T(8,128)(2,1)S(1)} %collective-permute-done.18.refs_2_), channel_id=1, source_target_pairs={{0,1},{1,0},{2,3},{3,2},{4,5},{5,4},{6,7},{7,6},{8,9},{9,8},{10,11... | collective-permute-start | bytes 1572872 | tf_op jit(solution)/shard_map/ppermute | solution.py:436
  97.7 9.8 %collective-permute-start.22 = (bf16[512,512]{1,0:T(8,128)(2,1)S(1)}, bf16[512,512]{1,0:T(8,128)(2,1)S(1)}, u32[]{:S(2)}, u32[]{:S(2)}) collective-permute-start(bf16[512,512]{1,0:T(8,128)(2,1)S(1)} %collective-permute-done.21.refs_0_), channel_id=1, source_target_pairs={{0,1},{1,0},{2,3},{3,2},{4,5},{5,4},{6,7},{7,6},{8,9},{9,8},{10,11... | collective-permute-start | bytes 1572872 | tf_op jit(solution)/shard_map/ppermute | solution.py:436
  97.7 9.8 %collective-permute-start.24 = (bf16[512,512]{1,0:T(8,128)(2,1)S(1)}, bf16[512,512]{1,0:T(8,128)(2,1)S(1)}, u32[]{:S(2)}, u32[]{:S(2)}) collective-permute-start(bf16[512,512]{1,0:T(8,128)(2,1)S(1)} %collective-permute-done.23.refs_2_), channel_id=1, source_target_pairs={{0,1},{1,0},{2,3},{3,2},{4,5},{5,4},{6,7},{7,6},{8,9},{9,8},{10,11... | collective-permute-start | bytes 1572872 | tf_op jit(solution)/shard_map/ppermute | solution.py:436
  101.6 7.3 %collective-permute-start.17 = (bf16[512,512]{1,0:T(8,128)(2,1)S(1)}, bf16[512,512]{1,0:T(8,128)(2,1)S(1)}, u32[]{:S(2)}, u32[]{:S(2)}) collective-permute-start(bf16[512,512]{1,0:T(8,128)(2,1)S(1)} %collective-permute-done.16.refs_0_), channel_id=1, source_target_pairs={{0,1},{1,0},{2,3},{3,2},{4,5},{5,4},{6,7},{7,6},{8,9},{9,8},{10,11... | collective-permute-start | bytes 1572872 | tf_op jit(solution)/shard_map/ppermute | solution.py:436
  103.3 5.6 %collective-permute-start.20 = (bf16[512,512]{1,0:T(8,128)(2,1)S(1)}, bf16[512,512]{1,0:T(8,128)(2,1)S(1)}, u32[]{:S(2)}, u32[]{:S(2)}) collective-permute-start(bf16[512,512]{1,0:T(8,128)(2,1)S(1)} %collective-permute-done.19.refs_2_), channel_id=1, source_target_pairs={{0,1},{1,0},{2,3},{3,2},{4,5},{5,4},{6,7},{7,6},{8,9},{9,8},{10,11... | collective-permute-start | bytes 1572872 | tf_op jit(solution)/shard_map/ppermute | solution.py:436
  (3 other events, 23.2 us)
